TPU v7x, 16 devices: a 4x2x1 block of a 4x4x8 slice. The times are simulated.
16 devices in a mesh: dp: 2 (over y, z), sp: 8 (over x, core).
Axes of the slice: x: 4, y: 2, z: 1, core: 2. Of those that a mesh axis runs over, the one named last changes fastest.
The devices are a block of a 4x4x8 slice.
Arguments:
- dec_hidden: bfloat16 [8192, 768], P(('dp', 'sp')), parts along dimension 0
- memory: bfloat16 [4096, 768], P(('dp', 'sp')), parts along dimension 0
- mem_len: int32 [2], P('dp'), parts along dimension 0
- gain_self: bfloat16 [2, 768], replicated
- gain_cross: bfloat16 [2, 768], replicated
- gain_mlp: bfloat16 [2, 768], replicated
- self_q: bfloat16 [2, 768, 768], replicated
- self_k: bfloat16 [2, 768, 768], replicated
- self_v: bfloat16 [2, 768, 768], replicated
- self_o: bfloat16 [2, 768, 768], replicated
- cross_q: bfloat16 [2, 768, 768], replicated
- cross_k: bfloat16 [2, 768, 128], replicated
- cross_v: bfloat16 [2, 768, 128], replicated
- cross_o: bfloat16 [2, 768, 768], replicated
- mlp_gate: bfloat16 [2, 768, 2048], replicated
- mlp_up: bfloat16 [2, 768, 2048], replicated
- mlp_down: bfloat16 [2, 2048, 768], replicated
Outputs:
- output: bfloat16 [8192, 768], P(('dp', 'sp')), parts along dimension 0
There are 2 independent parts. A program takes and returns all parts, laid end to end along the dimension named above; an argument that names none is the same for every part.
All inputs are finite; a program needn't handle non-finite values.
Results may differ from a plain program's by a relative error of at most 0.0139901.
Values are sent between devices in bfloat16 or wider.
A program may use at most 768 MiB of HBM per device.

v0:
```python
import jax
import jax.numpy as jnp
from jax import lax
from jax.sharding import PartitionSpec as P

HEAD_DIM = 64
NORM_EPS = 1e-6
MASK_VALUE = -1e30
ATT_SCALE = HEAD_DIM ** -0.5


def rms_norm(values, gain_vec):
    val32 = values.astype(jnp.float32)
    inv_rms = lax.rsqrt(jnp.mean(val32 * val32, axis=-1, keepdims=True) + NORM_EPS)
    return (val32 * inv_rms * gain_vec.astype(jnp.float32)).astype(jnp.bfloat16)


def project(rows, weight):
    return jnp.dot(rows, weight, preferred_element_type=jnp.float32)


def add_residual(hidden, update):
    return (hidden.astype(jnp.float32) + update).astype(jnp.bfloat16)


def self_attention(normed, w_query, w_key, w_value, w_out, causal):
    tq_dev, d_model = normed.shape
    n_heads = d_model // HEAD_DIM
    q_rows = project(normed, w_query).astype(jnp.bfloat16).reshape(tq_dev, n_heads, HEAD_DIM)
    k_rows = project(normed, w_key).astype(jnp.bfloat16)
    v_rows = project(normed, w_value).astype(jnp.bfloat16)
    k_all = lax.all_gather(k_rows, "sp", axis=0, tiled=True).reshape(-1, n_heads, HEAD_DIM)
    v_all = lax.all_gather(v_rows, "sp", axis=0, tiled=True).reshape(-1, n_heads, HEAD_DIM)
    scores = jnp.einsum("thd,shd->hts", q_rows, k_all, preferred_element_type=jnp.float32) * ATT_SCALE
    scores = jnp.where(causal, scores, MASK_VALUE)
    exp_vals = jnp.exp(scores - jnp.max(scores, axis=-1, keepdims=True))
    row_sum = jnp.sum(exp_vals, axis=-1)
    weighted = jnp.einsum("hts,shd->thd", exp_vals.astype(jnp.bfloat16), v_all, preferred_element_type=jnp.float32)
    attn_out = (weighted / row_sum.T[:, :, None]).astype(jnp.bfloat16).reshape(tq_dev, d_model)
    return project(attn_out, w_out)


def cross_attention(normed, memory, mem_valid, x_query, x_key, x_value, x_out):
    tq_dev, d_model = normed.shape
    tm_dev = memory.shape[0]
    n_heads = d_model // HEAD_DIM
    kv_heads = x_key.shape[-1] // HEAD_DIM
    group_size = n_heads // kv_heads
    q_rows = project(normed, x_query).astype(jnp.bfloat16)
    q_all = lax.all_gather(q_rows, "sp", axis=0, tiled=True)
    tq_all = q_all.shape[0]
    q_all = q_all.reshape(tq_all, kv_heads, group_size, HEAD_DIM)
    mem_k = project(memory, x_key).astype(jnp.bfloat16).reshape(tm_dev, kv_heads, HEAD_DIM)
    mem_v = project(memory, x_value).astype(jnp.bfloat16).reshape(tm_dev, kv_heads, HEAD_DIM)
    scores = jnp.einsum("uhse,the->hsut", q_all, mem_k, preferred_element_type=jnp.float32) * ATT_SCALE
    scores = jnp.where(mem_valid, scores, MASK_VALUE)
    loc_max = jnp.max(scores, axis=-1)
    exp_vals = jnp.exp(scores - loc_max[..., None])
    loc_sum = jnp.sum(exp_vals, axis=-1)
    loc_out = jnp.einsum("hsut,the->uhse", exp_vals.astype(jnp.bfloat16), mem_v, preferred_element_type=jnp.float32)
    glob_max = lax.pmax(loc_max, "sp")
    rescale = jnp.exp(loc_max - glob_max)
    num_part = (loc_out * rescale.transpose(2, 0, 1)[..., None]).reshape(tq_all, d_model)
    den_part = (loc_sum * rescale).transpose(2, 0, 1).reshape(tq_all, n_heads)
    packed = jnp.concatenate([num_part, den_part], axis=1)
    own_rows = lax.psum_scatter(packed, "sp", scatter_dimension=0, tiled=True)
    num_own = own_rows[:, :d_model].reshape(tq_dev, n_heads, HEAD_DIM)
    den_own = own_rows[:, d_model:]
    attn_out = (num_own / den_own[:, :, None]).astype(jnp.bfloat16).reshape(tq_dev, d_model)
    return project(attn_out, x_out)


def solution(mesh):
    n_seq = mesh.shape["sp"]
    row_spec = P(("dp", "sp"), None)

    def device_fn(dec_hidden, memory, mem_len, gain_self, gain_cross, gain_mlp, self_q, self_k, self_v, self_o, cross_q, cross_k, cross_v, cross_o, mlp_gate, mlp_up, mlp_down):
        tq_dev = dec_hidden.shape[0]
        tm_dev = memory.shape[0]
        seq_idx = lax.axis_index("sp")
        q_pos = seq_idx * tq_dev + jnp.arange(tq_dev)
        causal = q_pos[:, None] >= jnp.arange(tq_dev * n_seq)[None, :]
        mem_valid = seq_idx * tm_dev + jnp.arange(tm_dev) < mem_len[0]
        hidden = dec_hidden
        for layer_idx in range(gain_self.shape[0]):
            normed = rms_norm(hidden, gain_self[layer_idx])
            hidden = add_residual(hidden, self_attention(normed, self_q[layer_idx], self_k[layer_idx], self_v[layer_idx], self_o[layer_idx], causal))
            normed = rms_norm(hidden, gain_cross[layer_idx])
            hidden = add_residual(hidden, cross_attention(normed, memory, mem_valid, cross_q[layer_idx], cross_k[layer_idx], cross_v[layer_idx], cross_o[layer_idx]))
            normed = rms_norm(hidden, gain_mlp[layer_idx])
            act_vals = (jax.nn.silu(project(normed, mlp_gate[layer_idx])) * project(normed, mlp_up[layer_idx])).astype(jnp.bfloat16)
            hidden = add_residual(hidden, project(act_vals, mlp_down[layer_idx]))
        return hidden

    return jax.shard_map(device_fn, mesh=mesh, in_specs=(row_spec, row_spec, P("dp")) + (P(),) * 14, out_specs=row_spec, check_vma=False)
```

profile of v0, /device:TPU:112, one launch (start us, length us, event | category | flops | bytes accessed | tf_op | source)
XLA Modules:
  0.0 850.2 jit_solution(6192861690721933066)
XLA Ops:
  6.6 1.4 convert_reduce_fusion.2
  8.0 1.4 fusion.44
  9.3 3.2 convolution_convert_fusion.5
  12.7 3.0 convolution_convert_fusion.7
  15.9 2.1 convolution_convert_fusion.6
  18.0 0.3 copy.29
  18.3 0.6 convert_reduce_fusion.1
  18.9 1.6 iota_compare_fusion
  20.5 31.7 %all-gather.9.cloned.1.call-done = bf16[4096,768]{1,0:T(8,128)(2,1)} async-done(((bf16[512,768]{1,0:T(8,128)(2,1)}), bf16[4096,768]{1,0:T(8,128)(2,1)}) %all-gather.9.cloned.1.call-update) | async-done | bytes 6291472 | tf_op jit(solution)/shard_map/all_gather | solution.py:32
  52.2 9.0 %copy.30 = bf16[4096,768]{0,1:T(8,128)(2,1)} copy(bf16[4096,768]{1,0:T(8,128)(2,1)} %all-gather.9.cloned.1.call-done) | data formatting | bytes 12582912 | tf_op jit(solution)/shard_map/all_gather | solution.py:32
  61.2 38.3 %fusion = (f32[12,512]{1,0:T(8,128)S(1)}, f32[12,512,4096]{2,1,0:T(8,128)}) fusion(pred[512,4096]{1,0:T(8,128)(4,1)S(1)} %iota_compare_fusion, bf16[512,12,64]{0,2,1:T(8,128)(2,1)S(1)} %bitcast.202, bf16[4096,12,64]{0,2,1:T(8,128)(2,1)} %bitcast.196), kind=kOutput, calls=%fused_computation.4 | convolution fusion | flops 3296716800 | bytes 109862912 | tf_op jit(solution)/shard_map/thd,shd->hts/dot_general | solution.py:34
  99.5 31.5 %fusion.2 = f32[12,512]{1,0:T(8,128)S(1)} fusion(f32[12,512,4096]{2,1,0:T(8,128)} %get-tuple-element.16, f32[12,512]{1,0:T(8,128)S(1)} %get-tuple-element.15, pred[512,4096]{1,0:T(8,128)(4,1)S(1)} %iota_compare_fusion), kind=kLoop, calls=%fused_computation.6 | loop fusion | flops 100657152 | bytes 102809600 | tf_op jit(solution)/shard_map/reduce_sum | solution.py:37
  131.0 8.9 %copy.28 = bf16[4096,768]{0,1:T(8,128)(2,1)} copy(bf16[4096,768]{1,0:T(8,128)(2,1)} %all-gather.7.cloned.1.call-done) | data formatting | bytes 12582912 | tf_op jit(solution)/shard_map/all_gather | solution.py:33
  139.8 37.4 %fusion.71 = bf16[512,12,64]{0,2,1:T(8,128)(2,1)} fusion(bf16[4096,12,64]{0,2,1:T(8,128)(2,1)} %bitcast.201, f32[12,512,4096]{2,1,0:T(8,128)} %get-tuple-element.16, f32[12,512]{1,0:T(8,128)S(1)} %get-tuple-element.15, pred[512,4096]{1,0:T(8,128)(4,1)S(1)} %iota_compare_fusion, f32[512,12]{0,1:T(8,128)S(1)} %bitcast.209), kind=kOutput, calls=%fused_computation.102 | convolution fusion | flops 3322675200 | bytes 109887488 | tf_op jit(solution)/shard_map/hts,shd->thd/dot_general | solution.py:38
  177.2 2.6 fusion.48
  179.8 0.9 copy-done.18
  180.7 1.7 convolution_convert_fusion.4
  183.5 0.3 convolution_convert_fusion.10
  183.8 0.9 convolution_convert_fusion.11
  184.7 34.6 %all-gather.11.cloned.1.call-done = bf16[4096,768]{1,0:T(8,128)(2,1)} async-done(((bf16[512,768]{1,0:T(8,128)(2,1)}), bf16[4096,768]{1,0:T(8,128)(2,1)}) %all-gather.11.cloned.1.call-update) | async-done | bytes 6291472 | tf_op jit(solution)/shard_map/all_gather | solution.py:50
  219.3 8.7 %copy.31 = bf16[4096,768]{0,1:T(8,128)(2,1)} copy(bf16[4096,768]{1,0:T(8,128)(2,1)} %all-gather.11.cloned.1.call-done) | data formatting | bytes 12582912 | tf_op jit(solution)/shard_map/all_gather | solution.py:50
  228.0 23.1 %bitcast_reduce_fusion.1 = (f32[2,6,4096]{2,1,0:T(8,128)}, f32[2,256,4096,6]{2,1,3,0:T(8,128)}) fusion(pred[256]{0:T(512)(128)(4,1)S(1)} %add_compare_fusion, bf16[256,2,64,1]{0,2,3,1:T(8,128)(2,1)S(1)} %bitcast.204, bf16[4096,2,6,64]{0,3,2,1:T(8,128)(2,1)} %bitcast.194), kind=kOutput, calls=%fused_computation.14 | convolution fusion | flops 1648312320 | bytes 56885504 | tf_op jit(solution)/shard_map/uhse,the->hsut/dot_general | solution.py:55
  251.2 22.2 %fusion.14 = f32[2,6,4096]{2,1,0:T(8,128)S(1)} fusion(f32[2,256,4096,6]{2,1,3,0:T(8,128)} %get-tuple-element.20, f32[2,6,4096]{2,1,0:T(8,128)} %get-tuple-element.19, pred[256]{0:T(512)(128)(4,1)S(1)} %add_compare_fusion), kind=kLoop, calls=%fused_computation.22 | loop fusion | flops 50282496 | bytes 50725120 | tf_op jit(solution)/shard_map/reduce_sum | solution.py:59
  273.5 30.1 %all-reduce.3.cloned.1.call-done = f32[2,6,4096]{2,1,0:T(8,128)} async-done(((f32[2,6,4096]{2,1,0:T(8,128)}), f32[2,6,4096]{2,1,0:T(8,128)}) %all-reduce.3.cloned.1.call-update) | async-done | bytes 196624 | tf_op jit(solution)/shard_map/pmax | solution.py:61
  303.5 1.0 fusion.134
  304.6 24.3 %bitcast_multiply_fusion.1 = f32[4096,2,6,64]{0,3,2,1:T(8,128)} fusion(bf16[256,2,64,1]{0,2,3,1:T(8,128)(2,1)} %bitcast.207, f32[2,256,4096,6]{2,1,3,0:T(8,128)} %get-tuple-element.20, f32[2,6,4096]{2,1,0:T(8,128)S(1)} %copy-done.2, pred[256]{0:T(512)(128)(4,1)S(1)} %add_compare_fusion, f32[4096,2,6]{0,2,1:T(8,128)S(1)} %get-tuple-element.13), kind=kOutput, calls=%fused_computation.33 | convolution fusion | flops 1664090112 | bytes 63373568 | tf_op jit(solution)/shard_map/hsut,the->uhse/dot_general | solution.py:60
  328.9 11.3 %pad_maximum_fusion = f32[4096,780]{0,1:T(8,128)} fusion(f32[4096,12]{0,1:T(8,128)S(1)} %reshape.130, f32[4096,768]{0,1:T(8,128)} %bitcast.199), kind=kLoop, calls=%fused_computation.30 | loop fusion | flops 3194880 | bytes 25559040 | tf_op jit(solution)/shard_map/concatenate | solution.py:65
  340.3 0.5 all-gather.15.cloned.1.call-start
  340.9 0.6 convert_reduce_fusion
  341.5 67.4 %reduce-scatter.3.cloned.1.call-done = f32[512,780]{0,1:T(8,128)} async-done(((f32[4096,780]{0,1:T(8,128)}), f32[512,780]{0,1:T(8,128)}) %reduce-scatter.3.cloned.1.call-update) | async-done | bytes 1597456 | tf_op jit(solution)/shard_map/reduce_scatter | solution.py:66
  408.9 0.8 slice.129
  409.7 1.6 fusion.69
  411.3 2.2 fusion.52
  413.6 0.9 copy-done.21
  414.4 5.7 fusion.36
  420.1 8.3 fusion.56
  428.4 3.3 convolution_convert_fusion.1
  431.9 3.0 convolution_convert_fusion.3
  435.0 3.0 convolution_convert_fusion.2
  438.0 1.4 copy.34
  439.4 28.8 %all-gather.15.cloned.1.call-done = bf16[4096,768]{1,0:T(8,128)(2,1)} async-done(((bf16[512,768]{1,0:T(8,128)(2,1)}), bf16[4096,768]{1,0:T(8,128)(2,1)}) %all-gather.15.cloned.1.call-update) | async-done | bytes 6291472 | tf_op jit(solution)/shard_map/all_gather | solution.py:32
  468.1 9.0 %copy.35 = bf16[4096,768]{0,1:T(8,128)(2,1)} copy(bf16[4096,768]{1,0:T(8,128)(2,1)} %all-gather.15.cloned.1.call-done) | data formatting | bytes 12582912 | tf_op jit(solution)/shard_map/all_gather | solution.py:32
  477.2 38.3 %fusion.1 = (f32[12,512]{1,0:T(8,128)S(1)}, f32[12,512,4096]{2,1,0:T(8,128)}) fusion(pred[512,4096]{1,0:T(8,128)(4,1)S(1)} %iota_compare_fusion, bf16[512,12,64]{0,2,1:T(8,128)(2,1)S(1)} %bitcast.203, bf16[4096,12,64]{0,2,1:T(8,128)(2,1)} %bitcast.197), kind=kOutput, calls=%fused_computation.5 | convolution fusion | flops 3296716800 | bytes 109862912 | tf_op jit(solution)/shard_map/thd,shd->hts/dot_general | solution.py:34
  515.4 31.5 %fusion.4 = f32[12,512]{1,0:T(8,128)S(1)} fusion(f32[12,512,4096]{2,1,0:T(8,128)} %get-tuple-element.26, f32[12,512]{1,0:T(8,128)S(1)} %get-tuple-element.25, pred[512,4096]{1,0:T(8,128)(4,1)S(1)} %iota_compare_fusion), kind=kLoop, calls=%fused_computation.8 | loop fusion | flops 100657152 | bytes 102809600 | tf_op jit(solution)/shard_map/reduce_sum | solution.py:37
  547.0 8.9 %copy.33 = bf16[4096,768]{0,1:T(8,128)(2,1)} copy(bf16[4096,768]{1,0:T(8,128)(2,1)} %all-gather.13.cloned.1.call-done) | data formatting | bytes 12582912 | tf_op jit(solution)/shard_map/all_gather | solution.py:33
  555.8 37.3 %fusion.70 = bf16[512,12,64]{0,2,1:T(8,128)(2,1)} fusion(bf16[4096,12,64]{0,2,1:T(8,128)(2,1)} %bitcast.200, f32[12,512,4096]{2,1,0:T(8,128)} %get-tuple-element.26, f32[12,512]{1,0:T(8,128)S(1)} %get-tuple-element.25, pred[512,4096]{1,0:T(8,128)(4,1)S(1)} %iota_compare_fusion, f32[512,12]{0,1:T(8,128)S(1)} %bitcast.208), kind=kOutput, calls=%fused_computation.100 | convolution fusion | flops 3322675200 | bytes 109887488 | tf_op jit(solution)/shard_map/hts,shd->thd/dot_general | solution.py:38
  593.1 2.8 fusion.60
  596.0 1.7 convolution_convert_fusion
  598.1 0.3 convolution_convert_fusion.8
  598.4 0.3 convolution_convert_fusion.9
  598.7 35.9 %all-gather.17.cloned.1.call-done = bf16[4096,768]{1,0:T(8,128)(2,1)} async-done(((bf16[512,768]{1,0:T(8,128)(2,1)}), bf16[4096,768]{1,0:T(8,128)(2,1)}) %all-gather.17.cloned.1.call-update) | async-done | bytes 6291472 | tf_op jit(solution)/shard_map/all_gather | solution.py:50
  634.6 8.7 %copy.36 = bf16[4096,768]{0,1:T(8,128)(2,1)} copy(bf16[4096,768]{1,0:T(8,128)(2,1)} %all-gather.17.cloned.1.call-done) | data formatting | bytes 12582912 | tf_op jit(solution)/shard_map/all_gather | solution.py:50
  643.3 23.1 %bitcast_reduce_fusion = (f32[2,6,4096]{2,1,0:T(8,128)}, f32[2,256,4096,6]{2,1,3,0:T(8,128)}) fusion(pred[256]{0:T(512)(128)(4,1)S(1)} %copy-done.10, bf16[256,2,64,1]{0,2,3,1:T(8,128)(2,1)S(1)} %bitcast.205, bf16[4096,2,6,64]{0,3,2,1:T(8,128)(2,1)} %bitcast.195), kind=kOutput, calls=%fused_computation.11 | convolution fusion | flops 1648312320 | bytes 56885504 | tf_op jit(solution)/shard_map/uhse,the->hsut/dot_general | solution.py:55
  666.5 22.2 %fusion.16 = f32[2,6,4096]{2,1,0:T(8,128)S(1)} fusion(f32[2,256,4096,6]{2,1,3,0:T(8,128)} %get-tuple-element.30, f32[2,6,4096]{2,1,0:T(8,128)} %get-tuple-element.29, pred[256]{0:T(512)(128)(4,1)S(1)} %copy-done.10), kind=kLoop, calls=%fused_computation.24 | loop fusion | flops 50282496 | bytes 50725120 | tf_op jit(solution)/shard_map/reduce_sum | solution.py:59
  688.8 30.1 %all-reduce.5.cloned.1.call-done = f32[2,6,4096]{2,1,0:T(8,128)} async-done(((f32[2,6,4096]{2,1,0:T(8,128)}), f32[2,6,4096]{2,1,0:T(8,128)}) %all-reduce.5.cloned.1.call-update) | async-done | bytes 196624 | tf_op jit(solution)/shard_map/pmax | solution.py:61
  718.9 1.0 fusion.135
  719.9 24.3 %bitcast_multiply_fusion = f32[4096,2,6,64]{0,3,2,1:T(8,128)} fusion(bf16[256,2,64,1]{0,2,3,1:T(8,128)(2,1)S(1)} %bitcast.206, f32[2,256,4096,6]{2,1,3,0:T(8,128)} %get-tuple-element.30, f32[2,6,4096]{2,1,0:T(8,128)S(1)} %copy-done.1, pred[256]{0:T(512)(128)(4,1)S(1)} %copy-done.10, f32[4096,2,6]{0,2,1:T(8,128)S(1)} %get-tuple-element.11), kind=kOutput, calls=%fused_computation.32 | convolution fusion | flops 1664090112 | bytes 63373568 | tf_op jit(solution)/shard_map/hsut,the->uhse/dot_general | solution.py:60
  744.2 11.3 %pad_maximum_fusion.1 = f32[4096,780]{0,1:T(8,128)} fusion(f32[4096,12]{0,1:T(8,128)S(1)} %reshape.139, f32[4096,768]{0,1:T(8,128)} %bitcast.198), kind=kLoop, calls=%fused_computation.31 | loop fusion | flops 3194880 | bytes 25559040 | tf_op jit(solution)/shard_map/concatenate | solution.py:65
  755.6 68.6 %reduce-scatter.5.cloned.1.call-done = f32[512,780]{0,1:T(8,128)} async-done(((f32[4096,780]{0,1:T(8,128)}), f32[512,780]{0,1:T(8,128)}) %reduce-scatter.5.cloned.1.call-update) | async-done | bytes 1597456 | tf_op jit(solution)/shard_map/reduce_scatter | solution.py:66
  824.2 0.8 slice.131
  825.0 1.6 fusion.68
  826.6 2.2 fusion.64
  828.8 5.7 fusion.31
  834.5 8.6 %fusion.67 = bf16[512,768]{1,0:T(8,128)(2,1)} fusion(bf16[512,768]{1,0:T(8,128)(2,1)S(1)} %get-tuple-element.32, bf16[2,2048,768]{2,1,0:T(8,128)(2,1)} %param.33, f32[512,2048]{1,0:T(8,128)} %fusion.31, bf16[2,768,2048]{2,1,0:T(8,128)(2,1)} %param.32, f32[768]{0:T(1024)S(1)} %copy-done.15, f32[512]{0:T(512)S(1)} %add_rsqrt_fusion), kind=kOutput, calls=%fused_computation.94 | convolution fusion | flops 3230269440 | bytes 12851200 | tf_op jit(solution)/shard_map/dot_general | solution.py:19
  (73 shorter events, 1.9 us)
Async XLA Ops:
  6.5 176.9 %copy-start = (bf16[256,768]{1,0:T(8,128)(2,1)S(1)}, bf16[256,768]{1,0:T(8,128)(2,1)}, u32[]{:S(2)}) copy-start(bf16[256,768]{1,0:T(8,128)(2,1)} %param.18) | copy-start | bytes 1179652
  6.6 6.2 copy-start.3
  6.6 45.6 %all-gather.9.cloned.1.call-start = ((), (), s32[]{:S(2)}) async-start(), calls=%async_computation.3 | async-start | bytes 7077888 | tf_op jit(solution)/shard_map/all_gather | solution.py:32
  12.6 118.3 %all-gather.7.cloned.1.call-start = ((), (), s32[]{:S(2)}) async-start(), calls=%async_computation.2 | async-start | bytes 7077888 | tf_op jit(solution)/shard_map/all_gather | solution.py:33
  15.7 2.5 copy-start.11
  15.8 203.5 %all-gather.11.cloned.1.call-start = ((), (), s32[]{:S(2)}) async-start(), calls=%async_computation.4 | async-start | bytes 7077888 | tf_op jit(solution)/shard_map/all_gather | solution.py:50
  139.8 37.4 %copy-start.4 = (bf16[512,768]{1,0:T(8,128)(2,1)S(1)}, bf16[512,768]{1,0:T(8,128)(2,1)}, u32[]{:S(2)}) copy-start(bf16[512,768]{1,0:T(8,128)(2,1)} %param.17) | copy-start | bytes 2359300
  177.2 3.5 copy-start.16
  179.8 0.9 copy-start.18
  179.8 3.6 copy-start.5
  179.8 4.0 copy-start.7
  182.5 121.1 %all-reduce.3.cloned.1.call-start = ((), (), s32[]{:S(2)}) async-start(), calls=%async_computation.5 | async-start | bytes 524288 | tf_op jit(solution)/shard_map/pmax | solution.py:61
  183.5 121.1 %copy-start.9 = (pred[256]{0:T(512)(128)(4,1)}, pred[256]{0:T(512)(128)(4,1)S(1)}, u32[]{:S(2)}) copy-start(pred[256]{0:T(512)(128)(4,1)S(1)} %add_compare_fusion) | copy-start | bytes 772
  251.2 157.8 %reduce-scatter.3.cloned.1.call-start = ((), (), s32[]{:S(2)}) async-start(), calls=%async_computation.6 | async-start | bytes 14450688 | tf_op jit(solution)/shard_map/reduce_scatter | solution.py:66
  251.2 52.3 %copy-start.2 = (f32[2,6,4096]{2,1,0:T(8,128)S(1)}, f32[2,6,4096]{2,1,0:T(8,128)}, u32[]{:S(2)}) copy-start(f32[2,6,4096]{2,1,0:T(8,128)} %get-tuple-element.19) | copy-start | bytes 589828
  340.2 0.7 copy-start.12
  340.2 71.1 %copy-start.19 = (bf16[512,768]{1,0:T(8,128)(2,1)S(1)}, bf16[512,768]{1,0:T(8,128)(2,1)}, u32[]{:S(2)}) copy-start(bf16[512,768]{1,0:T(8,128)(2,1)} %copy-done.18) | copy-start | bytes 2359300
  340.3 127.8 %all-gather.15.cloned.1.call-start = ((), (), s32[]{:S(2)}) async-start(), calls=%async_computation.8 | async-start | bytes 7077888 | tf_op jit(solution)/shard_map/all_gather | solution.py:32
  413.5 0.9 copy-start.21
  420.1 8.3 copy-start.13
  428.4 6.6 copy-start.20
  431.8 115.2 %all-gather.13.cloned.1.call-start = ((), (), s32[]{:S(2)}) async-start(), calls=%async_computation.7 | async-start | bytes 7077888 | tf_op jit(solution)/shard_map/all_gather | solution.py:33
  434.9 199.7 %all-gather.17.cloned.1.call-start = ((), (), s32[]{:S(2)}) async-start(), calls=%async_computation.9 | async-start | bytes 7077888 | tf_op jit(solution)/shard_map/all_gather | solution.py:50
  593.1 2.8 copy-start.14
  593.1 2.9 copy-start.17
  593.1 4.9 copy-start.6
  595.9 2.4 copy-start.8
  597.8 121.1 %all-reduce.5.cloned.1.call-start = ((), (), s32[]{:S(2)}) async-start(), calls=%async_computation.10 | async-start | bytes 524288 | tf_op jit(solution)/shard_map/pmax | solution.py:61
  598.7 44.7 %copy-start.10 = (pred[256]{0:T(512)(128)(4,1)S(1)}, pred[256]{0:T(512)(128)(4,1)}, u32[]{:S(2)}) copy-start(pred[256]{0:T(512)(128)(4,1)} %copy-done.9) | copy-start | bytes 772
  666.5 157.8 %reduce-scatter.5.cloned.1.call-start = ((), (), s32[]{:S(2)}) async-start(), calls=%async_computation.11 | async-start | bytes 14450688 | tf_op jit(solution)/shard_map/reduce_scatter | solution.py:66
  666.5 52.3 %copy-start.1 = (f32[2,6,4096]{2,1,0:T(8,128)S(1)}, f32[2,6,4096]{2,1,0:T(8,128)}, u32[]{:S(2)}) copy-start(f32[2,6,4096]{2,1,0:T(8,128)} %get-tuple-element.29) | copy-start | bytes 589828
  755.6 73.2 %copy-start.15 = (f32[768]{0:T(1024)S(1)}, f32[768]{0:T(1024)}, u32[]{:S(2)}) copy-start(f32[768]{0:T(1024)} %get-tuple-element.5) | copy-start | bytes 9220
Sparse Core Ops, SparseCore 0:
  12.8 39.3 all-gather.8
  53.7 36.6 all-gather.6
  182.6 36.6 all-gather.10
  251.3 52.2 all-reduce.2
  340.4 68.4 reduce-scatter.2
  431.9 36.1 all-gather.14
  469.7 36.6 all-gather.12
  597.9 36.6 all-gather.16
  666.6 52.2 all-reduce.4
  755.7 68.4 reduce-scatter.4
where the time goes:
time: 857 us; the launch traced here: 850 us
  waiting for transfers between devices  328 us (38%)
  matrix products  307 us (36%)
  other arithmetic  141 us (16%)
  local copies, waits for them, and re-layouts  58.4 us (7%)
  between operations  14.8 us (2%)
    reduce_scatter x2, waiting for transfers between devices, cross_attention(): own_rows = lax.psum_scatter(packed, 'sp', scatter_dimension=0, tiled=True)  136 us
    dot_general x2, matrix products, self_attention(): jnp.einsum('thd,shd->hts', q_rows, k_all, preferred_element_type=jnp.floa...  76.6 us
    dot_general x2, matrix products, self_attention(): jnp.einsum('hts,shd->thd', exp_vals.astype(jnp.bfloat16), v_all, preferre...  74.6 us
    all_gather x2, waiting for transfers between devices, cross_attention(): q_all = lax.all_gather(q_rows, 'sp', axis=0, tiled=True)  70.5 us
    reduce_sum x2, other arithmetic, self_attention(): row_sum = jnp.sum(exp_vals, axis=-1)  63 us
    dot_general x20, matrix products, project(): return jnp.dot(rows, weight, preferred_element_type=jnp.float32)  60.9 us
    all_gather x2, waiting for transfers between devices, self_attention(): lax.all_gather(k_rows, 'sp', axis=0, tiled=True)  60.4 us
    pmax x2, waiting for transfers between devices, cross_attention(): glob_max = lax.pmax(loc_max, 'sp')  60.2 us
  transfers between devices with their start and end apart: 10, of which 8 were waited for; matrix products, arithmetic and copies ran while one was open for 26% of the time, Pallas kernels for 0%

commit v1 on v0

v1 whole, which is shorter than its diff:
```python
import functools

import jax
import jax.numpy as jnp
from jax import lax
from jax.experimental import pallas as pl
from jax.experimental.pallas import tpu as pltpu
from jax.sharding import PartitionSpec as P

HEAD_DIM = 64
NORM_EPS = 1e-6
MASK_VALUE = -1e30
ATT_SCALE = HEAD_DIM ** -0.5
MAX_MEM_LEN = 1536
PAIR = 2 * HEAD_DIM
TILE = 256
CHUNK = 512
NN = (((1,), (0,)), ((), ()))
NT = (((1,), (1,)), ((), ()))
F32 = jnp.float32
BF16 = jnp.bfloat16
MESH = pl.DeviceIdType.MESH
VMEM_LIMIT = 60 * 1024 * 1024
ANY = pl.BlockSpec(memory_space=pl.ANY)
VMEM = pl.BlockSpec(memory_space=pltpu.VMEM)
SMEM = pl.BlockSpec(memory_space=pltpu.SMEM)


def rms_norm(val32, gain_row):
    inv_rms = lax.rsqrt(jnp.mean(val32 * val32, axis=-1, keepdims=True) + NORM_EPS)
    return (val32 * inv_rms * gain_row).astype(BF16)


def dot(lhs, rhs, dims=NN):
    return lax.dot_general(lhs, rhs, dims, preferred_element_type=F32)


def col_scores(k_val, q_val, buf, size, mask, m_prev, mc):
    s = dot(k_val, q_val)
    if mask is not None:
        s = jnp.where(mask, s, MASK_VALUE)
    buf[:size] = s
    mc[...] = jnp.maximum(m_prev, jnp.max(s, axis=0, keepdims=True))


def col_softmax(buf, size, mc, n, m_ref, l_ref):
    m_new = mc[...]
    alpha = jnp.exp(m_ref[n] - m_new)
    e = jnp.exp(buf[:size] - m_new)
    l_ref[n] = l_ref[n] * alpha + jnp.sum(e, axis=0, keepdims=True)
    m_ref[n] = m_new
    return e.astype(BF16), alpha


def layer_kernel(n_sp, n_layers, len_ref, hid_hbm, mem_hbm, gain_s, gain_c, gain_m, wq_hbm, wk_hbm, wv_hbm, wo_hbm, cq_hbm,
                 ck_hbm, cv_hbm, co_hbm, wg_hbm, wu_hbm, wd_hbm, out_ref,
                 y, h_own, h_rem, mem, ck, cv, mkv, mall, wq, wk, wv, wqt, wvt, wo, cq, co, wg, wu, wd,
                 qm, qc, k_s, vt_s, k_c, vt_c, m_ref, l_ref, acc, b0, b1, mc0, mc1, o_stage, o_full, act, gains,
                 w_sem, own_sem, ici_s, ici_r, d2d_s, d2d_r, mi_s, mi_r, mo_s, mo_r, md_s, md_r, o_sem):
    rows, d_model = y.shape
    half = rows // 2
    width = d_model // 2
    pairs = width // PAIR
    tiles = 2 * rows // TILE
    row_tiles = rows // TILE
    all_pairs = d_model // PAIR
    used, _, mrows, mcols = mall.shape
    mh = mrows // 2
    kv_dim = mcols // 2
    n_kv = kv_dim // HEAD_DIM
    group = all_pairs // n_kv
    ff = act.shape[1]
    n_chip = n_sp // 2
    me = lax.axis_index("sp")
    chip, core = me // 2, lax.rem(me, 2)
    other = 1 - core
    right, left = lax.rem(chip + 1, n_chip), lax.rem(chip + n_chip - 1, n_chip)
    opp = lax.rem(chip + 2, n_chip)
    partner = 2 * chip + other
    dev_r, dev_l = 2 * right + core, 2 * left + core

    def remote(src, dst, send, recv, dev):
        return pltpu.make_async_remote_copy(
            src_ref=src, dst_ref=dst, send_sem=send, recv_sem=recv, device_id={"sp": dev}, device_id_type=MESH)

    cols = pl.ds(pl.multiple_of(core * width, 128), width)
    own_rows = pl.ds(pl.multiple_of(core * rows, rows), rows)
    other_rows = pl.ds(pl.multiple_of(other * rows, rows), rows)
    mine = pl.ds(pl.multiple_of(core * half, half), half)

    def loads(layer):
        specs = [(wq_hbm.at[layer, :, cols], wq), (wk_hbm.at[layer, :, cols], wk), (wv_hbm.at[layer, :, cols], wv),
                 (wo_hbm.at[layer], wo), (cq_hbm.at[layer], cq), (co_hbm.at[layer], co), (wg_hbm.at[layer], wg),
                 (wu_hbm.at[layer], wu), (wd_hbm.at[layer], wd)]
        return [pltpu.make_async_copy(src, dst, w_sem.at[i]) for i, (src, dst) in enumerate(specs)]

    first = [pltpu.make_async_copy(src, dst, w_sem.at[9 + i])
             for i, (src, dst) in enumerate(((hid_hbm, y), (mem_hbm, mem), (ck_hbm, ck), (cv_hbm, cv)))]
    first[0].start()
    w_first = loads(0)
    for copy in (*w_first[:3], *first[1:], *w_first[3:]):
        copy.start()

    barrier = pltpu.get_barrier_semaphore()
    for dev in (dev_r, dev_l, partner):
        pl.semaphore_signal(barrier, inc=1, device_id={"sp": dev}, device_id_type=MESH)

    for i, ref in enumerate((gain_s, gain_c, gain_m)):
        for j in range(n_layers):
            gains[i, j] = ref[j:j + 1].astype(F32)

    first[0].wait()
    h_own[0, own_rows] = rms_norm(y[...].astype(F32), gains[0, 0])
    pl.semaphore_wait(barrier, 3)

    to_r, to_l = chip < right, chip < left
    b_to_l = to_l | (chip < opp)
    relay_a, relay_b = left < right, right < left
    need_l, need_r, need_o = left < chip, right < chip, opp < chip
    got_rb = need_r | relay_b
    need = (need_l, need_r, need_l, need_r, need_o, need_o)
    got = (need_l, got_rb, need_l, need_r, need_o, need_o)
    sent = (to_r, b_to_l, to_r, to_l)

    def row_copies(layer):
        own_a = h_own.at[layer, pl.ds(pl.multiple_of(core * rows, half), half)]
        own_b = h_own.at[layer, pl.ds(pl.multiple_of(core * rows + half, half), half)]
        slot = [h_rem.at[layer, i, mine] for i in range(6)]
        srcs = (own_a, own_b, own_b, own_a, slot[0], slot[1])
        ring = [remote(srcs[i], slot[i], ici_s.at[layer, i], ici_r.at[layer, i], dev_l if i % 2 else dev_r)
                for i in (0, 1)]
        ring += [remote(srcs[2], slot[2], ici_s.at[layer, 2], ici_r.at[layer, 2], dev_r),
                 remote(srcs[3], slot[3], ici_s.at[layer, 3], ici_r.at[layer, 3], dev_l),
                 remote(srcs[4], slot[4], ici_s.at[layer, 4], ici_r.at[layer, 4], dev_r),
                 remote(srcs[5], slot[5], ici_s.at[layer, 5], ici_r.at[layer, 5], dev_l)]
        fwd = [remote(slot[i], slot[i], d2d_s.at[layer, i], d2d_r.at[layer, i], partner) for i in range(6)]
        own = remote(h_own.at[layer, own_rows], h_own.at[layer, own_rows], own_sem.at[layer, 0], own_sem.at[layer, 1],
                     partner)
        return ring, fwd, own

    def when_start(cond, copy):
        @pl.when(cond)
        def _():
            copy.start()

    def when_sent(cond, copy):
        @pl.when(cond)
        def _():
            copy.wait_send()

    def when_recv(cond, copy):
        @pl.when(cond)
        def _():
            copy.wait_recv()

    has_m = 2 * chip < used
    has_l, has_r, has_o = 2 * left < used, 2 * right < used, 2 * opp < used

    def blk(who, core_of):
        return jnp.minimum(2 * who + core_of, used - 1)

    b_me, b_l, b_r, b_o = blk(chip, core), blk(left, core), blk(right, core), blk(opp, core)
    top, low = pl.ds(0, mh), pl.ds(mh, mh)
    m_own = [
        remote(mkv, mall.at[b_me], mi_s.at[0], mi_r.at[0], dev_r),
        remote(mkv, mall.at[b_me], mi_s.at[1], mi_r.at[1], dev_l),
        remote(mkv, mall.at[b_me], md_s.at[0], md_r.at[0], partner),
    ]
    m_relay = [
        remote(mall.at[b_l, :, top], mall.at[b_l, :, top], mo_s.at[0], mo_r.at[0], dev_r),
        remote(mall.at[b_r, :, low], mall.at[b_r, :, low], mo_s.at[1], mo_r.at[1], dev_l),
    ]
    m_fwd = [
        remote(mall.at[b_l], mall.at[b_l], md_s.at[1], md_r.at[1], partner),
        remote(mall.at[b_r], mall.at[b_r], md_s.at[2], md_r.at[2], partner),
        remote(mall.at[b_o, :, top], mall.at[b_o, :, top], md_s.at[3], md_r.at[3], partner),
        remote(mall.at[b_o, :, low], mall.at[b_o, :, low], md_s.at[4], md_r.at[4], partner),
    ]
    m_has = (has_l, has_r, has_o, has_o)

    def start_rows(layer):
        ring, _, own = row_copies(layer)
        own.start()
        when_start(sent[0], ring[0])
        when_start(sent[1], ring[1])

    start_rows(0)
    for copy in first[1:]:
        copy.wait()
    for i in range(n_layers):
        mkv[i, :, :kv_dim] = dot(mem[...], ck[i]).astype(BF16)
        mkv[i, :, kv_dim:] = dot(mem[...], cv[i]).astype(BF16)

    @pl.when(has_m)
    def _():
        mall[b_me] = mkv[...]

    qm[...] = jnp.zeros_like(qm)
    ones_row = (lax.broadcasted_iota(jnp.int32, (PAIR - HEAD_DIM, 2 * TILE), 0) == 0).astype(F32).astype(BF16)
    for n in range(qc.shape[0]):
        qc[n, HEAD_DIM:] = ones_row

    def reset():
        m_ref[...] = jnp.full_like(m_ref, MASK_VALUE)
        l_ref[...] = jnp.zeros_like(l_ref)
        acc[...] = jnp.zeros_like(acc)

    def scores_of(k_val, q_val, n, buf, mc, size=CHUNK, mask=None):
        col_scores(k_val, q_val, buf, size, mask, m_ref[n], mc)

    def softmax_of(vt_top, vt_low, n, buf, mc, size=CHUNK):
        e, alpha = col_softmax(buf, size, mc, n, m_ref, l_ref)
        acc[n, :HEAD_DIM] = acc[n, :HEAD_DIM] * alpha[:, :TILE] + dot(vt_top, e[:, :TILE])
        acc[n, HEAD_DIM:] = acc[n, HEAD_DIM:] * alpha[:, TILE:] + dot(vt_low, e[:, TILE:])

    def pipelined(count, unroll, item, scores, softmax):
        bufs, mcs = (b0, b1), (mc0, mc1)

        def at(i):
            return item(jnp.minimum(i, count - 1))

        scores(at(0), b0, mc0)

        def body(i, carry):
            for u in range(unroll):
                scores(at(unroll * i + u + 1), bufs[(u + 1) % 2], mcs[(u + 1) % 2])
                softmax(at(unroll * i + u), bufs[u % 2], mcs[u % 2])
            return carry

        lax.fori_loop(0, count // unroll, body, 0)

    def finish(n):
        inv = 1.0 / l_ref[n]
        val = jnp.concatenate([acc[n, :HEAD_DIM] * inv[:, :TILE], acc[n, HEAD_DIM:] * inv[:, TILE:]], axis=0)
        return val.astype(BF16).T

    def project_kv(h_chunk):
        k_val = dot(h_chunk, wk[...]).astype(BF16)
        v_val = dot(wvt[...], h_chunk, NT).astype(BF16)
        for p in range(pairs):
            k_s[p] = k_val[:, p * PAIR:(p + 1) * PAIR]
            vt_s[p] = v_val[p * PAIR:(p + 1) * PAIR]

    def self_scores(pn, buf, mc, size=CHUNK, mask=None):
        p, n = pn
        scores_of(k_s[p, :size], qm[n], n, buf, mc, size, mask)

    def self_softmax(pn, buf, mc, size=CHUNK):
        p, n = pn
        softmax_of(vt_s[p, :HEAD_DIM, :size], vt_s[p, HEAD_DIM:, :size], n, buf, mc, size)

    def attend(first_tile, n_tiles, unroll):
        def item(i):
            p = i // n_tiles
            return p, p * tiles + first_tile + lax.rem(i, n_tiles)

        pipelined(pairs * n_tiles, unroll, item, self_scores, self_softmax)

    def layer_body(layer, carry):
        ring, fwd, own = row_copies(layer)
        weights = loads(layer)
        reset()
        for copy in weights[:3]:
            copy.wait()
        wqt[...] = wq[...].T
        wvt[...] = wv[...].T
        own.wait_recv()

        def own_block(block, inner):
            h_blk = h_own[layer, pl.ds(pl.multiple_of(block * rows, rows), rows)]
            q_val = (dot(wqt[...], h_blk, NT).astype(BF16) * ATT_SCALE).astype(BF16)
            for p in range(pairs):
                for t in range(row_tiles):
                    n = p * tiles + block * row_tiles + t
                    span = slice(t * TILE, (t + 1) * TILE)
                    qm[n, :HEAD_DIM, :TILE] = q_val[p * PAIR:p * PAIR + HEAD_DIM, span]
                    qm[n, HEAD_DIM:, TILE:] = q_val[p * PAIR + HEAD_DIM:(p + 1) * PAIR, span]
            return inner

        lax.fori_loop(0, 2, own_block, 0)

        def own_keys(block, inner):
            project_kv(h_own[layer, pl.ds(pl.multiple_of(block * rows, rows), rows)])
            key = lax.broadcasted_iota(jnp.int32, (CHUNK, 2 * TILE), 0)
            query = lax.broadcasted_iota(jnp.int32, (CHUNK, 2 * TILE), 1) % TILE

            def diagonal(p, deep):
                n = p * tiles + block * row_tiles
                self_scores((p, n), b0, mc0, TILE, key[:TILE] <= query[:TILE])
                self_scores((p, n + 1), b1, mc1, CHUNK, key <= query + TILE)
                self_softmax((p, n), b0, mc0, TILE)
                self_softmax((p, n + 1), b1, mc1, CHUNK)
                return deep

            lax.fori_loop(0, pairs, diagonal, 0)

            @pl.when(block == 0)
            def _():
                attend(tiles // 2, tiles // 2, 2)

            return inner

        lax.fori_loop(0, 2, own_keys, 0)
        when_start(sent[2], ring[2])
        when_start(sent[3], ring[3])

        def take(i):
            when_recv(got[i], ring[i])
            if i == 0:
                when_start(relay_a, ring[4])
            if i == 1:
                when_start(relay_b, ring[5])
            when_start(need[i], fwd[i])

        def attend_two(stage, inner):
            @pl.when(stage == 0)
            def _():
                take(0)
                take(1)

                @pl.when(layer == 0)
                def _():
                    when_start(has_m, m_own[2])
                    when_start(has_m, m_own[0])
                    when_start(has_m, m_own[1])

                when_recv(need[0], fwd[0])
                when_recv(need[1], fwd[1])

            @pl.when(stage == 1)
            def _():
                take(2)
                take(3)
                when_recv(need[2], fwd[2])
                when_recv(need[3], fwd[3])

            @pl.when(stage == 2)
            def _():
                take(4)
                take(5)
                when_recv(need[4], fwd[4])
                when_recv(need[5], fwd[5])

            def one(i, deep):
                @pl.when((stage == 2) & (i == 1) & (layer == 0))
                def _():
                    when_recv(has_l, m_own[0])
                    when_start(has_l, m_relay[0])
                    when_start(has_l, m_fwd[0])
                    when_recv(has_r, m_own[1])
                    when_start(has_r, m_relay[1])
                    when_start(has_r, m_fwd[1])

                wanted = jnp.where(stage == 2, opp, jnp.where(i == 0, left, right)) < chip

                @pl.when(wanted)
                def _():
                    project_kv(h_rem[layer, 2 * stage + i])
                    attend(0, tiles, 4)

                return deep

            return lax.fori_loop(0, 2, one, inner)

        lax.fori_loop(0, 3, attend_two, 0)

        for block, dst in ((other, o_stage), (core, None)):
            for p in range(pairs):
                for t in range(row_tiles):
                    val = finish(p * tiles + block * row_tiles + t)
                    span = slice(t * TILE, (t + 1) * TILE)
                    if dst is not None:
                        dst[layer, span, p * PAIR:(p + 1) * PAIR] = val
                    else:
                        o_full[layer, core, span, p * PAIR:(p + 1) * PAIR] = val
        o_send = remote(o_stage.at[layer], o_full.at[layer, core], o_sem.at[layer, 0], o_sem.at[layer, 1], partner)
        o_send.start()

        @pl.when(layer + 1 < n_layers)
        def _():
            for copy in loads(layer + 1)[:3]:
                copy.start()

        @pl.when(layer == 0)
        def _():
            when_recv(has_o, m_relay[0])
            when_start(has_o, m_fwd[2])
            when_recv(has_o, m_relay[1])
            when_start(has_o, m_fwd[3])
            when_recv(has_m, m_own[2])
            for cond, copy in zip(m_has, m_fwd):
                when_recv(cond, copy)
            for copy in m_own:
                when_sent(has_m, copy)
            when_sent(has_l, m_relay[0])
            when_sent(has_r, m_relay[1])
            for cond, copy in zip(m_has, m_fwd):
                when_sent(cond, copy)

        reset()
        mem_len = len_ref[0]
        for b in range(used):
            span = slice(b * mrows, (b + 1) * mrows)
            vt = mall[b, layer, :, kv_dim:].T
            pos = lax.broadcasted_iota(jnp.int32, (mrows, HEAD_DIM), 0) + b * mrows
            lane = lax.broadcasted_iota(jnp.int32, (mrows, HEAD_DIM), 1)
            bias = jnp.where((pos >= mem_len) & (lane == 0), MASK_VALUE, 0.0).astype(BF16)
            for g in range(n_kv):
                k_c[g, span, :HEAD_DIM] = mall[b, layer, :, g * HEAD_DIM:(g + 1) * HEAD_DIM]
                k_c[g, span, HEAD_DIM:] = bias
                vt_c[g, :, span] = vt[g * HEAD_DIM:(g + 1) * HEAD_DIM]

        o_send.wait_recv()
        weights[3].wait()
        upd = dot(o_full[layer, 0], wo[:width]) + dot(o_full[layer, 1], wo[width:])
        y1 = (y[...].astype(F32) + upd).astype(BF16)
        y[...] = y1
        h = rms_norm(y1.astype(F32), gains[1, layer])
        weights[4].wait()
        q_val = (dot(h, cq[...]).astype(BF16) * ATT_SCALE).astype(BF16)
        for p in range(all_pairs):
            qt = q_val[:, p * PAIR:(p + 1) * PAIR].T
            for t in range(row_tiles):
                span = slice(t * TILE, (t + 1) * TILE)
                qc[p * row_tiles + t, :HEAD_DIM, :TILE] = qt[:HEAD_DIM, span]
                qc[p * row_tiles + t, :HEAD_DIM, TILE:] = qt[HEAD_DIM:, span]

        def chunk(c, inner):
            off = pl.multiple_of(c * CHUNK, CHUNK)

            def item(n):
                return n // (row_tiles * group), n

            def scores(gn, buf, mc):
                g, n = gn
                scores_of(k_c[g, pl.ds(off, CHUNK)], qc[n], n, buf, mc)

            def softmax(gn, buf, mc):
                g, n = gn
                vt = vt_c[g, :, pl.ds(off, CHUNK)]
                softmax_of(vt, vt, n, buf, mc)

            pipelined(all_pairs * row_tiles, 4, item, scores, softmax)
            return inner

        lax.fori_loop(0, used * mrows // CHUNK, chunk, 0)
        for p in range(all_pairs):
            for t in range(row_tiles):
                o_stage_c[t * TILE:(t + 1) * TILE, p * PAIR:(p + 1) * PAIR] = finish(p * row_tiles + t)
        weights[5].wait()
        y2 = (y[...].astype(F32) + dot(o_stage_c[...], co[...])).astype(BF16)
        y[...] = y2
        h = rms_norm(y2.astype(F32), gains[2, layer])
        weights[6].wait()
        weights[7].wait()
        for c in range(0, ff, CHUNK):
            gate = dot(h, wg[:, c:c + CHUNK])
            act[:, c:c + CHUNK] = (jax.nn.silu(gate) * dot(h, wu[:, c:c + CHUNK])).astype(BF16)
        weights[8].wait()
        y3 = (y[...].astype(F32) + dot(act[...], wd[...])).astype(BF16)
        y[...] = y3

        @pl.when(layer + 1 < n_layers)
        def _():
            h_own[layer + 1, own_rows] = rms_norm(y3.astype(F32), gains[0, layer + 1])
            for copy in loads(layer + 1)[3:]:
                copy.start()
            start_rows(layer + 1)

        own.wait_send()
        o_send.wait_send()
        for cond, copy in zip((*sent, relay_a, relay_b), ring):
            when_sent(cond, copy)
        for cond, copy in zip(need, fwd):
            when_sent(cond, copy)
        return carry

    o_stage_c = act.at[:, :d_model]
    lax.fori_loop(0, n_layers, layer_body, 0)
    out_ref[...] = y[...]


def layers_call(n_sp, mem_len, hidden, memory, gain_self, gain_cross, gain_mlp, self_q, self_k, self_v, self_o, cross_q,
                cross_k, cross_v, cross_o, gate, up, down):
    rows, d_model = hidden.shape
    layers = gain_self.shape[0]
    width = d_model // 2
    ff = gate.shape[2]
    mrows, mcols = memory.shape[0], 2 * cross_k.shape[2]
    used = min(n_sp, pl.cdiv(MAX_MEM_LEN, mrows))
    n_kv = cross_k.shape[2] // HEAD_DIM
    pairs, tiles = width // PAIR, 2 * rows // TILE
    combos = pairs * tiles
    dma = pltpu.SemaphoreType.DMA
    return pl.pallas_call(
        functools.partial(layer_kernel, n_sp, layers),
        out_shape=jax.ShapeDtypeStruct((rows, d_model), BF16),
        in_specs=[SMEM, ANY, ANY, VMEM, VMEM, VMEM] + [ANY] * 11,
        out_specs=VMEM,
        scratch_shapes=[
            pltpu.VMEM((rows, d_model), BF16),
            pltpu.VMEM((layers, 2 * rows, d_model), BF16),
            pltpu.VMEM((layers, 6, rows, d_model), BF16),
            pltpu.VMEM((mrows, d_model), BF16),
            *[pltpu.VMEM(cross_k.shape, BF16)] * 2,
            pltpu.VMEM((layers, mrows, mcols), BF16),
            pltpu.VMEM((used, layers, mrows, mcols), BF16),
            *[pltpu.VMEM((d_model, width), BF16)] * 3,
            *[pltpu.VMEM((width, d_model), BF16)] * 2,
            *[pltpu.VMEM((d_model, d_model), BF16)] * 3,
            *[pltpu.VMEM((d_model, ff), BF16)] * 2,
            pltpu.VMEM((ff, d_model), BF16),
            *[pltpu.VMEM((combos, PAIR, 2 * TILE), BF16)] * 2,
            pltpu.VMEM((pairs, CHUNK, PAIR), BF16),
            pltpu.VMEM((pairs, PAIR, CHUNK), BF16),
            pltpu.VMEM((n_kv, used * mrows, PAIR), BF16),
            pltpu.VMEM((n_kv, HEAD_DIM, used * mrows), BF16),
            *[pltpu.VMEM((combos, 1, 2 * TILE), F32)] * 2,
            pltpu.VMEM((combos, PAIR, TILE), F32),
            *[pltpu.VMEM((CHUNK, 2 * TILE), F32)] * 2,
            *[pltpu.VMEM((1, 2 * TILE), F32)] * 2,
            pltpu.VMEM((layers, rows, width), BF16),
            pltpu.VMEM((layers, 2, rows, width), BF16),
            pltpu.VMEM((rows, ff), BF16),
            pltpu.VMEM((3, layers, 1, d_model), F32),
            dma((13,)), dma((layers, 2)), *[dma((layers, 6))] * 4,
            *[dma((2,))] * 4, *[dma((5,))] * 2, dma((layers, 2)),
        ],
        compiler_params=pltpu.CompilerParams(collective_id=0, has_side_effects=True, vmem_limit_bytes=VMEM_LIMIT),
        name="layers",
    )(mem_len, hidden, memory, gain_self, gain_cross, gain_mlp, self_q, self_k, self_v, self_o, cross_q, cross_k, cross_v,
      cross_o, gate, up, down)


def solution(mesh):
    n_sp = mesh.shape["sp"]
    row_spec = P(("dp", "sp"), None)

    def device_fn(dec_hidden, memory, mem_len, *weights):
        return layers_call(n_sp, mem_len, dec_hidden, memory, *weights)

    return jax.shard_map(device_fn, mesh=mesh, in_specs=(row_spec, row_spec, P("dp")) + (P(),) * 14,
                         out_specs=row_spec, check_vma=False)
```

time: 857 us -> 147 us (0.17)
  the two profiles are of different devices: /device:TPU:112 before, /device:TPU:119 now
where the time goes in v1:
time: 147 us
  Pallas kernels  144 us (98%)
  local copies, waits for them, and re-layouts  2.06 us (1%)
    pallas_call x1, Pallas kernels, layers_call(): pl.pallas_call(functools.partial(layer_kernel, n_sp, layers), out_shape=j...  144 us

profile of v1, /device:TPU:119, one launch (start us, length us, event | category | flops | bytes accessed | tf_op | source)
XLA Modules:
  0.0 146.6 jit_solution(10270895075121258321)
XLA Ops:
  0.7 143.9 %layers.1 = bf16[512,768]{1,0:T(8,128)(2,1)} custom-call(s32[1]{0:T(128)S(6)} %copy.19.len_ref, bf16[512,768]{1,0:T(8,128)(2,1)} %hid_hbm.1, bf16[256,768]{1,0:T(8,128)(2,1)} %mem_hbm.1, bf16[2,768]{1,0:T(2,128)(2,1)} %gain_s.1, bf16[2,768]{1,0:T(2,128)(2,1)} %gain_c.1, bf16[2,768]{1,0:T(2,128)(2,1)} %gain_m.1, bf16[2,768,768]{2,1,0:T(8,128)(2,1)} %wq_hbm.1, ...), custom_call_target="tpu_custom_call" | custom-call | tf_op jit(solution)/shard_map/layers/pallas_call | solution.py:495
  144.5 2.1 %copy.20 = bf16[512,768]{1,0:T(8,128)(2,1)} copy(bf16[512,768]{1,0:T(8,128)(2,1)} %layers.1) | data formatting | bytes 1572864

commit v2 on v1

--- a/solution.py
+++ b/solution.py
@@ -86,7 +86,6 @@
     cols = pl.ds(pl.multiple_of(core * width, 128), width)
     own_rows = pl.ds(pl.multiple_of(core * rows, rows), rows)
     other_rows = pl.ds(pl.multiple_of(other * rows, rows), rows)
-    mine = pl.ds(pl.multiple_of(core * half, half), half)
 
     def loads(layer):
         specs = [(wq_hbm.at[layer, :, cols], wq), (wk_hbm.at[layer, :, cols], wk), (wv_hbm.at[layer, :, cols], wv),
@@ -125,7 +124,7 @@
     def row_copies(layer):
         own_a = h_own.at[layer, pl.ds(pl.multiple_of(core * rows, half), half)]
         own_b = h_own.at[layer, pl.ds(pl.multiple_of(core * rows + half, half), half)]
-        slot = [h_rem.at[layer, i, mine] for i in range(6)]
+        slot = [h_rem.at[layer, i, core] for i in range(6)]
         srcs = (own_a, own_b, own_b, own_a, slot[0], slot[1])
         ring = [remote(srcs[i], slot[i], ici_s.at[layer, i], ici_r.at[layer, i], dev_l if i % 2 else dev_r)
                 for i in (0, 1)]
@@ -187,12 +186,12 @@
     start_rows(0)
     for copy in first[1:]:
         copy.wait()
-    for i in range(n_layers):
-        mkv[i, :, :kv_dim] = dot(mem[...], ck[i]).astype(BF16)
-        mkv[i, :, kv_dim:] = dot(mem[...], cv[i]).astype(BF16)
 
     @pl.when(has_m)
     def _():
+        for i in range(n_layers):
+            mkv[i, :, :kv_dim] = dot(mem[...], ck[i]).astype(BF16)
+            mkv[i, :, kv_dim:] = dot(mem[...], cv[i]).astype(BF16)
         mall[b_me] = mkv[...]
 
     qm[...] = jnp.zeros_like(qm)
@@ -234,12 +233,15 @@
         val = jnp.concatenate([acc[n, :HEAD_DIM] * inv[:, :TILE], acc[n, HEAD_DIM:] * inv[:, TILE:]], axis=0)
         return val.astype(BF16).T
 
-    def project_kv(h_chunk):
-        k_val = dot(h_chunk, wk[...]).astype(BF16)
-        v_val = dot(wvt[...], h_chunk, NT).astype(BF16)
-        for p in range(pairs):
-            k_s[p] = k_val[:, p * PAIR:(p + 1) * PAIR]
-            vt_s[p] = v_val[p * PAIR:(p + 1) * PAIR]
+    def project_kv(pieces):
+        size = CHUNK // len(pieces)
+        for i, piece in enumerate(pieces):
+            span = slice(i * size, (i + 1) * size)
+            k_val = dot(piece, wk[...]).astype(BF16)
+            v_val = dot(wvt[...], piece, NT).astype(BF16)
+            for p in range(pairs):
+                k_s[p, span] = k_val[:, p * PAIR:(p + 1) * PAIR]
+                vt_s[p, :, span] = v_val[p * PAIR:(p + 1) * PAIR]
 
     def self_scores(pn, buf, mc, size=CHUNK, mask=None):
         p, n = pn
@@ -264,9 +266,14 @@
             copy.wait()
         wqt[...] = wq[...].T
         wvt[...] = wv[...].T
-        own.wait_recv()
-
-        def own_block(block, inner):
+
+        def own_block(i, inner):
+            block = jnp.where(i == 0, core, other)
+
+            @pl.when(i == 1)
+            def _():
+                own.wait_recv()
+
             h_blk = h_own[layer, pl.ds(pl.multiple_of(block * rows, rows), rows)]
             q_val = (dot(wqt[...], h_blk, NT).astype(BF16) * ATT_SCALE).astype(BF16)
             for p in range(pairs):
@@ -280,7 +287,7 @@
         lax.fori_loop(0, 2, own_block, 0)
 
         def own_keys(block, inner):
-            project_kv(h_own[layer, pl.ds(pl.multiple_of(block * rows, rows), rows)])
+            project_kv([h_own[layer, pl.ds(pl.multiple_of(block * rows, rows), rows)]])
             key = lax.broadcasted_iota(jnp.int32, (CHUNK, 2 * TILE), 0)
             query = lax.broadcasted_iota(jnp.int32, (CHUNK, 2 * TILE), 1) % TILE
 
@@ -297,12 +304,12 @@
             @pl.when(block == 0)
             def _():
                 attend(tiles // 2, tiles // 2, 2)
+                when_start(sent[2], ring[2])
+                when_start(sent[3], ring[3])
 
             return inner
 
         lax.fori_loop(0, 2, own_keys, 0)
-        when_start(sent[2], ring[2])
-        when_start(sent[3], ring[3])
 
         def take(i):
             when_recv(got[i], ring[i])
@@ -324,24 +331,29 @@
                     when_start(has_m, m_own[0])
                     when_start(has_m, m_own[1])
 
-                when_recv(need[0], fwd[0])
-                when_recv(need[1], fwd[1])
 
             @pl.when(stage == 1)
             def _():
                 take(2)
                 take(3)
-                when_recv(need[2], fwd[2])
-                when_recv(need[3], fwd[3])
 
             @pl.when(stage == 2)
             def _():
                 take(4)
                 take(5)
-                when_recv(need[4], fwd[4])
-                when_recv(need[5], fwd[5])
+
+            any_need = jnp.where(stage == 2, opp, left) < chip
+            both = jnp.where(stage == 2, opp, right) < chip
 
             def one(i, deep):
+                @pl.when(i == 1)
+                def _():
+                    for j in range(3):
+                        @pl.when(stage == j)
+                        def _(j=j):
+                            when_recv(need[2 * j], fwd[2 * j])
+                            when_recv(need[2 * j + 1], fwd[2 * j + 1])
+
                 @pl.when((stage == 2) & (i == 1) & (layer == 0))
                 def _():
                     when_recv(has_l, m_own[0])
@@ -351,12 +363,13 @@
                     when_start(has_r, m_relay[1])
                     when_start(has_r, m_fwd[1])
 
-                wanted = jnp.where(stage == 2, opp, jnp.where(i == 0, left, right)) < chip
-
-                @pl.when(wanted)
+                @pl.when(any_need & ((i == 1) | both))
                 def _():
-                    project_kv(h_rem[layer, 2 * stage + i])
-                    attend(0, tiles, 4)
+                    from_a = jnp.where((i == 1) & both, other, core)
+                    from_b = jnp.where(i == 1, other, core)
+                    slot_b = jnp.where(both, 2 * stage + 1, 2 * stage)
+                    project_kv([h_rem[layer, 2 * stage, from_a], h_rem[layer, slot_b, from_b]])
+                    attend(0, tiles, 6)
 
                 return deep
 
@@ -440,7 +453,7 @@
                 vt = vt_c[g, :, pl.ds(off, CHUNK)]
                 softmax_of(vt, vt, n, buf, mc)
 
-            pipelined(all_pairs * row_tiles, 4, item, scores, softmax)
+            pipelined(all_pairs * row_tiles, 6, item, scores, softmax)
             return inner
 
         lax.fori_loop(0, used * mrows // CHUNK, chunk, 0)
@@ -500,7 +513,7 @@
         scratch_shapes=[
             pltpu.VMEM((rows, d_model), BF16),
             pltpu.VMEM((layers, 2 * rows, d_model), BF16),
-            pltpu.VMEM((layers, 6, rows, d_model), BF16),
+            pltpu.VMEM((layers, 6, 2, rows // 2, d_model), BF16),
             pltpu.VMEM((mrows, d_model), BF16),
             *[pltpu.VMEM(cross_k.shape, BF16)] * 2,
             pltpu.VMEM((layers, mrows, mcols), BF16),

time: 147 us -> 132 us (0.90)
  Pallas kernels: 144 us -> 129 us
    pallas_call x1, Pallas kernels: 144 us -> 129 us  [layers_call(): pl.pallas_call(functools.partial(layer_kernel, n_sp, layers), out_shape=j...]
where the time goes in v2:
time: 132 us
  Pallas kernels  129 us (98%)
  local copies, waits for them, and re-layouts  2.06 us (2%)
    pallas_call x1, Pallas kernels, layers_call(): pl.pallas_call(functools.partial(layer_kernel, n_sp, layers), out_shape=j...  129 us

profile of v2, /device:TPU:119, one launch (start us, length us, event | category | flops | bytes accessed | tf_op | source)
XLA Modules:
  0.0 132.0 jit_solution(11212519539870523538)
XLA Ops:
  0.7 129.3 %layers.1 = bf16[512,768]{1,0:T(8,128)(2,1)} custom-call(s32[1]{0:T(128)S(6)} %copy.19.len_ref, bf16[512,768]{1,0:T(8,128)(2,1)} %hid_hbm.1, bf16[256,768]{1,0:T(8,128)(2,1)} %mem_hbm.1, bf16[2,768]{1,0:T(2,128)(2,1)} %gain_s.1, bf16[2,768]{1,0:T(2,128)(2,1)} %gain_c.1, bf16[2,768]{1,0:T(2,128)(2,1)} %gain_m.1, bf16[2,768,768]{2,1,0:T(8,128)(2,1)} %wq_hbm.1, ...), custom_call_target="tpu_custom_call" | custom-call | tf_op jit(solution)/shard_map/layers/pallas_call | solution.py:508
  129.9 2.1 %copy.20 = bf16[512,768]{1,0:T(8,128)(2,1)} copy(bf16[512,768]{1,0:T(8,128)(2,1)} %layers.1) | data formatting | bytes 1572864

commit v3 on v2

--- a/solution.py
+++ b/solution.py
@@ -12,6 +12,7 @@
 MASK_VALUE = -1e30
 ATT_SCALE = HEAD_DIM ** -0.5
 MAX_MEM_LEN = 1536
+HANDED = 128
 PAIR = 2 * HEAD_DIM
 TILE = 256
 CHUNK = 512
@@ -35,20 +36,21 @@
     return lax.dot_general(lhs, rhs, dims, preferred_element_type=F32)
 
 
-def col_scores(k_val, q_val, buf, size, mask, m_prev, mc):
+def col_scores(k_val, q_val, buf, size, mask, n, m_ref, mc):
+    width = q_val.shape[1]
     s = dot(k_val, q_val)
     if mask is not None:
         s = jnp.where(mask, s, MASK_VALUE)
-    buf[:size] = s
-    mc[...] = jnp.maximum(m_prev, jnp.max(s, axis=0, keepdims=True))
-
-
-def col_softmax(buf, size, mc, n, m_ref, l_ref):
-    m_new = mc[...]
-    alpha = jnp.exp(m_ref[n] - m_new)
-    e = jnp.exp(buf[:size] - m_new)
-    l_ref[n] = l_ref[n] * alpha + jnp.sum(e, axis=0, keepdims=True)
-    m_ref[n] = m_new
+    buf[:size, :width] = s
+    mc[:, :width] = jnp.maximum(m_ref[n, :, :width], jnp.max(s, axis=0, keepdims=True))
+
+
+def col_softmax(buf, size, width, mc, n, m_ref, l_ref):
+    m_new = mc[:, :width]
+    alpha = jnp.exp(m_ref[n, :, :width] - m_new)
+    e = jnp.exp(buf[:size, :width] - m_new)
+    l_ref[n, :, :width] = l_ref[n, :, :width] * alpha + jnp.sum(e, axis=0, keepdims=True)
+    m_ref[n, :, :width] = m_new
     return e.astype(BF16), alpha
 
 
@@ -56,7 +58,9 @@
                  ck_hbm, cv_hbm, co_hbm, wg_hbm, wu_hbm, wd_hbm, out_ref,
                  y, h_own, h_rem, mem, ck, cv, mkv, mall, wq, wk, wv, wqt, wvt, wo, cq, co, wg, wu, wd,
                  qm, qc, k_s, vt_s, k_c, vt_c, m_ref, l_ref, acc, b0, b1, mc0, mc1, o_stage, o_full, act, gains,
-                 w_sem, own_sem, ici_s, ici_r, d2d_s, d2d_r, mi_s, mi_r, mo_s, mo_r, md_s, md_r, o_sem):
+                 y_give, y_take, o_take, y_back, y_done, o_part,
+                 w_sem, own_sem, ici_s, ici_r, d2d_s, d2d_r, mi_s, mi_r, mo_s, mo_r, md_s, md_r, o_sem,
+                 give_s, give_r):
     rows, d_model = y.shape
     half = rows // 2
     width = d_model // 2
@@ -78,6 +82,9 @@
     opp = lax.rem(chip + 2, n_chip)
     partner = 2 * chip + other
     dev_r, dev_l = 2 * right + core, 2 * left + core
+    gives = 2 * chip >= n_chip
+    mate = 2 * (n_chip - 1 - chip) + core
+    keep = rows - HANDED
 
     def remote(src, dst, send, recv, dev):
         return pltpu.make_async_remote_copy(
@@ -136,6 +143,17 @@
         own = remote(h_own.at[layer, own_rows], h_own.at[layer, own_rows], own_sem.at[layer, 0], own_sem.at[layer, 1],
                      partner)
         return ring, fwd, own
+
+    def give_copies(layer):
+        return [remote(y_give.at[layer], y_take.at[layer], give_s.at[layer, 0], give_r.at[layer, 0], mate),
+                remote(o_full.at[layer, :, pl.ds(keep, HANDED)], o_take.at[layer], give_s.at[layer, 1],
+                       give_r.at[layer, 1], mate),
+                remote(y_back.at[layer], y_done.at[layer], give_s.at[layer, 2], give_r.at[layer, 2], mate)]
+
+    def give_y(layer):
+        @pl.when(gives)
+        def _():
+            give_copies(layer)[0].start()
 
     def when_start(cond, copy):
         @pl.when(cond)
@@ -183,7 +201,9 @@
         when_start(sent[0], ring[0])
         when_start(sent[1], ring[1])
 
+    y_give[0] = y[keep:]
     start_rows(0)
+    give_y(0)
     for copy in first[1:]:
         copy.wait()
 
@@ -195,7 +215,7 @@
         mall[b_me] = mkv[...]
 
     qm[...] = jnp.zeros_like(qm)
-    ones_row = (lax.broadcasted_iota(jnp.int32, (PAIR - HEAD_DIM, 2 * TILE), 0) == 0).astype(F32).astype(BF16)
+    ones_row = (lax.broadcasted_iota(jnp.int32, (PAIR - HEAD_DIM, qc.shape[2]), 0) == 0).astype(F32).astype(BF16)
     for n in range(qc.shape[0]):
         qc[n, HEAD_DIM:] = ones_row
 
@@ -203,14 +223,6 @@
         m_ref[...] = jnp.full_like(m_ref, MASK_VALUE)
         l_ref[...] = jnp.zeros_like(l_ref)
         acc[...] = jnp.zeros_like(acc)
-
-    def scores_of(k_val, q_val, n, buf, mc, size=CHUNK, mask=None):
-        col_scores(k_val, q_val, buf, size, mask, m_ref[n], mc)
-
-    def softmax_of(vt_top, vt_low, n, buf, mc, size=CHUNK):
-        e, alpha = col_softmax(buf, size, mc, n, m_ref, l_ref)
-        acc[n, :HEAD_DIM] = acc[n, :HEAD_DIM] * alpha[:, :TILE] + dot(vt_top, e[:, :TILE])
-        acc[n, HEAD_DIM:] = acc[n, HEAD_DIM:] * alpha[:, TILE:] + dot(vt_low, e[:, TILE:])
 
     def pipelined(count, unroll, item, scores, softmax):
         bufs, mcs = (b0, b1), (mc0, mc1)
@@ -228,10 +240,9 @@
 
         lax.fori_loop(0, count // unroll, body, 0)
 
-    def finish(n):
-        inv = 1.0 / l_ref[n]
-        val = jnp.concatenate([acc[n, :HEAD_DIM] * inv[:, :TILE], acc[n, HEAD_DIM:] * inv[:, TILE:]], axis=0)
-        return val.astype(BF16).T
+    def finish(n, m):
+        val = acc[n, :, :2 * m] * (1.0 / l_ref[n, :, :2 * m])
+        return jnp.concatenate([val[:, :m], val[:, m:]], axis=0).astype(BF16).T
 
     def project_kv(pieces):
         size = CHUNK // len(pieces)
@@ -245,11 +256,14 @@
 
     def self_scores(pn, buf, mc, size=CHUNK, mask=None):
         p, n = pn
-        scores_of(k_s[p, :size], qm[n], n, buf, mc, size, mask)
+        col_scores(k_s[p, :size], qm[n], buf, size, mask, n, m_ref, mc)
 
     def self_softmax(pn, buf, mc, size=CHUNK):
         p, n = pn
-        softmax_of(vt_s[p, :HEAD_DIM, :size], vt_s[p, HEAD_DIM:, :size], n, buf, mc, size)
+        w = 2 * TILE
+        e, alpha = col_softmax(buf, size, w, mc, n, m_ref, l_ref)
+        acc[n, :, :TILE] = acc[n, :, :TILE] * alpha[:, :TILE] + dot(vt_s[p, :HEAD_DIM, :size], e[:, :TILE])
+        acc[n, :, TILE:w] = acc[n, :, TILE:w] * alpha[:, TILE:] + dot(vt_s[p, HEAD_DIM:, :size], e[:, TILE:])
 
     def attend(first_tile, n_tiles, unroll):
         def item(i):
@@ -257,6 +271,51 @@
             return p, p * tiles + first_tile + lax.rem(i, n_tiles)
 
         pipelined(pairs * n_tiles, unroll, item, self_scores, self_softmax)
+
+    def rest_of_layer(layer, y_rows, o_rows, m):
+        w = 2 * m
+        m_ref[:all_pairs, :, :w] = jnp.full((all_pairs, 1, w), MASK_VALUE, F32)
+        l_ref[:all_pairs, :, :w] = jnp.zeros((all_pairs, 1, w), F32)
+        acc[:all_pairs, :, :w] = jnp.zeros((all_pairs, HEAD_DIM, w), F32)
+        upd = dot(o_rows[0], wo[:width]) + dot(o_rows[1], wo[width:])
+        y1 = (y_rows[...].astype(F32) + upd).astype(BF16)
+        y_rows[...] = y1
+        h = rms_norm(y1.astype(F32), gains[1, layer])
+        q_val = (dot(h, cq[...]).astype(BF16) * ATT_SCALE).astype(BF16)
+        for p in range(all_pairs):
+            qt = q_val[:, p * PAIR:(p + 1) * PAIR].T
+            qc[p, :HEAD_DIM, :m] = qt[:HEAD_DIM]
+            qc[p, :HEAD_DIM, m:w] = qt[HEAD_DIM:]
+
+        def chunk(c, inner):
+            off = pl.multiple_of(c * CHUNK, CHUNK)
+
+            def item(n):
+                return n // group, n
+
+            def scores(gn, buf, mc):
+                g, n = gn
+                col_scores(k_c[g, pl.ds(off, CHUNK)], qc[n, :, :w], buf, CHUNK, None, n, m_ref, mc)
+
+            def softmax(gn, buf, mc):
+                g, n = gn
+                e, alpha = col_softmax(buf, CHUNK, w, mc, n, m_ref, l_ref)
+                acc[n, :, :w] = acc[n, :, :w] * alpha + dot(vt_c[g, :, pl.ds(off, CHUNK)], e)
+
+            pipelined(all_pairs, all_pairs, item, scores, softmax)
+            return inner
+
+        lax.fori_loop(0, used * mrows // CHUNK, chunk, 0)
+        o2 = act.at[:m, :d_model]
+        for p in range(all_pairs):
+            o2[:, p * PAIR:(p + 1) * PAIR] = finish(p, m)
+        y2 = (y_rows[...].astype(F32) + dot(o2[...], co[...])).astype(BF16)
+        y_rows[...] = y2
+        h = rms_norm(y2.astype(F32), gains[2, layer])
+        for c in range(0, ff, CHUNK):
+            gate = dot(h, wg[:, c:c + CHUNK])
+            act[:m, c:c + CHUNK] = (jax.nn.silu(gate) * dot(h, wu[:, c:c + CHUNK])).astype(BF16)
+        y_rows[...] = (y_rows[...].astype(F32) + dot(act[:m], wd[...])).astype(BF16)
 
     def layer_body(layer, carry):
         ring, fwd, own = row_copies(layer)
@@ -380,7 +439,7 @@
         for block, dst in ((other, o_stage), (core, None)):
             for p in range(pairs):
                 for t in range(row_tiles):
-                    val = finish(p * tiles + block * row_tiles + t)
+                    val = finish(p * tiles + block * row_tiles + t, TILE)
                     span = slice(t * TILE, (t + 1) * TILE)
                     if dst is not None:
                         dst[layer, span, p * PAIR:(p + 1) * PAIR] = val
@@ -410,7 +469,6 @@
             for cond, copy in zip(m_has, m_fwd):
                 when_sent(cond, copy)
 
-        reset()
         mem_len = len_ref[0]
         for b in range(used):
             span = slice(b * mrows, (b + 1) * mrows)
@@ -424,61 +482,68 @@
                 vt_c[g, :, span] = vt[g * HEAD_DIM:(g + 1) * HEAD_DIM]
 
         o_send.wait_recv()
-        weights[3].wait()
-        upd = dot(o_full[layer, 0], wo[:width]) + dot(o_full[layer, 1], wo[width:])
-        y1 = (y[...].astype(F32) + upd).astype(BF16)
-        y[...] = y1
-        h = rms_norm(y1.astype(F32), gains[1, layer])
-        weights[4].wait()
-        q_val = (dot(h, cq[...]).astype(BF16) * ATT_SCALE).astype(BF16)
-        for p in range(all_pairs):
-            qt = q_val[:, p * PAIR:(p + 1) * PAIR].T
-            for t in range(row_tiles):
-                span = slice(t * TILE, (t + 1) * TILE)
-                qc[p * row_tiles + t, :HEAD_DIM, :TILE] = qt[:HEAD_DIM, span]
-                qc[p * row_tiles + t, :HEAD_DIM, TILE:] = qt[HEAD_DIM:, span]
-
-        def chunk(c, inner):
-            off = pl.multiple_of(c * CHUNK, CHUNK)
-
-            def item(n):
-                return n // (row_tiles * group), n
-
-            def scores(gn, buf, mc):
-                g, n = gn
-                scores_of(k_c[g, pl.ds(off, CHUNK)], qc[n], n, buf, mc)
-
-            def softmax(gn, buf, mc):
-                g, n = gn
-                vt = vt_c[g, :, pl.ds(off, CHUNK)]
-                softmax_of(vt, vt, n, buf, mc)
-
-            pipelined(all_pairs * row_tiles, 6, item, scores, softmax)
+        y_copy, o_copy, back_copy = give_copies(layer)
+        when_start(gives, o_copy)
+        for copy in weights[3:]:
+            copy.wait()
+        rest_of_layer(layer, y.at[:keep], o_full.at[layer, :, pl.ds(0, keep)], keep)
+
+        def next_rows(span):
+            h_own[layer + 1, pl.ds(core * rows + span.start, span.stop - span.start)] = rms_norm(
+                y[span].astype(F32), gains[0, layer + 1])
+
+        @pl.when(layer + 1 < n_layers)
+        def _():
+            next_rows(slice(0, keep))
+
+        def next_start():
+            @pl.when(layer + 1 < n_layers)
+            def _():
+                next_rows(slice(keep, rows))
+                y_give[layer + 1] = y[keep:]
+                start_rows(layer + 1)
+                give_y(layer + 1)
+
+        def handed(i, inner):
+            @pl.when(i == 0)
+            def _():
+                y_back[layer] = y[keep:]
+                o_part[...] = o_full[layer, :, keep:]
+
+            @pl.when(i == 1)
+            def _():
+                y_copy.wait_recv()
+                o_copy.wait_recv()
+                y_back[layer] = y_take[layer]
+                o_part[...] = o_take[layer]
+
+            rest_of_layer(layer, y_back.at[layer], o_part, HANDED)
+
+            @pl.when(i == 0)
+            def _():
+                y[keep:] = y_back[layer]
+                next_start()
+
             return inner
 
-        lax.fori_loop(0, used * mrows // CHUNK, chunk, 0)
-        for p in range(all_pairs):
-            for t in range(row_tiles):
-                o_stage_c[t * TILE:(t + 1) * TILE, p * PAIR:(p + 1) * PAIR] = finish(p * row_tiles + t)
-        weights[5].wait()
-        y2 = (y[...].astype(F32) + dot(o_stage_c[...], co[...])).astype(BF16)
-        y[...] = y2
-        h = rms_norm(y2.astype(F32), gains[2, layer])
-        weights[6].wait()
-        weights[7].wait()
-        for c in range(0, ff, CHUNK):
-            gate = dot(h, wg[:, c:c + CHUNK])
-            act[:, c:c + CHUNK] = (jax.nn.silu(gate) * dot(h, wu[:, c:c + CHUNK])).astype(BF16)
-        weights[8].wait()
-        y3 = (y[...].astype(F32) + dot(act[...], wd[...])).astype(BF16)
-        y[...] = y3
+        @pl.when(jnp.logical_not(gives))
+        def _():
+            lax.fori_loop(0, 2, handed, 0)
+            back_copy.start()
+            back_copy.wait_send()
+
+        @pl.when(gives)
+        def _():
+            back_copy.wait_recv()
+            y[keep:] = y_done[layer]
+            next_start()
+            y_copy.wait_send()
+            o_copy.wait_send()
 
         @pl.when(layer + 1 < n_layers)
         def _():
-            h_own[layer + 1, own_rows] = rms_norm(y3.astype(F32), gains[0, layer + 1])
             for copy in loads(layer + 1)[3:]:
                 copy.start()
-            start_rows(layer + 1)
 
         own.wait_send()
         o_send.wait_send()
@@ -488,7 +553,6 @@
             when_sent(cond, copy)
         return carry
 
-    o_stage_c = act.at[:, :d_model]
     lax.fori_loop(0, n_layers, layer_body, 0)
     out_ref[...] = y[...]
 
@@ -504,6 +568,7 @@
     n_kv = cross_k.shape[2] // HEAD_DIM
     pairs, tiles = width // PAIR, 2 * rows // TILE
     combos = pairs * tiles
+    wide = max(2 * TILE, 2 * (rows - HANDED))
     dma = pltpu.SemaphoreType.DMA
     return pl.pallas_call(
         functools.partial(layer_kernel, n_sp, layers),
@@ -523,21 +588,26 @@
             *[pltpu.VMEM((d_model, d_model), BF16)] * 3,
             *[pltpu.VMEM((d_model, ff), BF16)] * 2,
             pltpu.VMEM((ff, d_model), BF16),
-            *[pltpu.VMEM((combos, PAIR, 2 * TILE), BF16)] * 2,
+            pltpu.VMEM((combos, PAIR, 2 * TILE), BF16),
+            pltpu.VMEM((2 * pairs, PAIR, wide), BF16),
             pltpu.VMEM((pairs, CHUNK, PAIR), BF16),
             pltpu.VMEM((pairs, PAIR, CHUNK), BF16),
             pltpu.VMEM((n_kv, used * mrows, PAIR), BF16),
             pltpu.VMEM((n_kv, HEAD_DIM, used * mrows), BF16),
-            *[pltpu.VMEM((combos, 1, 2 * TILE), F32)] * 2,
-            pltpu.VMEM((combos, PAIR, TILE), F32),
-            *[pltpu.VMEM((CHUNK, 2 * TILE), F32)] * 2,
-            *[pltpu.VMEM((1, 2 * TILE), F32)] * 2,
+            *[pltpu.VMEM((combos, 1, wide), F32)] * 2,
+            pltpu.VMEM((combos, HEAD_DIM, wide), F32),
+            *[pltpu.VMEM((CHUNK, wide), F32)] * 2,
+            *[pltpu.VMEM((1, wide), F32)] * 2,
             pltpu.VMEM((layers, rows, width), BF16),
             pltpu.VMEM((layers, 2, rows, width), BF16),
             pltpu.VMEM((rows, ff), BF16),
             pltpu.VMEM((3, layers, 1, d_model), F32),
+            *[pltpu.VMEM((layers, HANDED, d_model), BF16)] * 2,
+            pltpu.VMEM((layers, 2, HANDED, width), BF16),
+            *[pltpu.VMEM((layers, HANDED, d_model), BF16)] * 2,
+            pltpu.VMEM((2, HANDED, width), BF16),
             dma((13,)), dma((layers, 2)), *[dma((layers, 6))] * 4,
-            *[dma((2,))] * 4, *[dma((5,))] * 2, dma((layers, 2)),
+            *[dma((2,))] * 4, *[dma((5,))] * 2, dma((layers, 2)), *[dma((layers, 3))] * 2,
         ],
         compiler_params=pltpu.CompilerParams(collective_id=0, has_side_effects=True, vmem_limit_bytes=VMEM_LIMIT),
         name="layers",

time: 132 us -> 147 us (1.11)
  the two profiles are of different devices: /device:TPU:119 before, /device:TPU:112 now
where the time goes in v3:
time: 147 us; the launch traced here: 146 us
  Pallas kernels  144 us (98%)
  local copies, waits for them, and re-layouts  2.06 us (1%)
    pallas_call x1, Pallas kernels, layers_call(): pl.pallas_call(functools.partial(layer_kernel, n_sp, layers), out_shape=j...  144 us

profile of v3, /device:TPU:112, one launch (start us, length us, event | category | flops | bytes accessed | tf_op | source)
XLA Modules:
  0.0 146.4 jit_solution(6599727948579299637)
XLA Ops:
  0.7 143.7 %layers.1 = bf16[512,768]{1,0:T(8,128)(2,1)} custom-call(s32[1]{0:T(128)S(6)} %copy.19.len_ref, bf16[512,768]{1,0:T(8,128)(2,1)} %hid_hbm.1, bf16[256,768]{1,0:T(8,128)(2,1)} %mem_hbm.1, bf16[2,768]{1,0:T(2,128)(2,1)} %gain_s.1, bf16[2,768]{1,0:T(2,128)(2,1)} %gain_c.1, bf16[2,768]{1,0:T(2,128)(2,1)} %gain_m.1, bf16[2,768,768]{2,1,0:T(8,128)(2,1)} %wq_hbm.1, ...), custom_call_target="tpu_custom_call" | custom-call | tf_op jit(solution)/shard_map/layers/pallas_call | solution.py:573
  144.3 2.1 %copy.20 = bf16[512,768]{1,0:T(8,128)(2,1)} copy(bf16[512,768]{1,0:T(8,128)(2,1)} %layers.1) | data formatting | bytes 1572864

commit v4 on v3

--- a/solution.py
+++ b/solution.py
@@ -82,9 +82,11 @@
     opp = lax.rem(chip + 2, n_chip)
     partner = 2 * chip + other
     dev_r, dev_l = 2 * right + core, 2 * left + core
-    gives = 2 * chip >= n_chip
+    last = n_chip - 1
+    gives, takes = chip == last, chip == 0
     mate = 2 * (n_chip - 1 - chip) + core
     keep = rows - HANDED
+    wide = 2 * keep
 
     def remote(src, dst, send, recv, dev):
         return pltpu.make_async_remote_copy(
@@ -183,9 +185,19 @@
         remote(mkv, mall.at[b_me], mi_s.at[1], mi_r.at[1], dev_l),
         remote(mkv, mall.at[b_me], md_s.at[0], md_r.at[0], partner),
     ]
-    m_relay = [
-        remote(mall.at[b_l, :, top], mall.at[b_l, :, top], mo_s.at[0], mo_r.at[0], dev_r),
-        remote(mall.at[b_r, :, low], mall.at[b_r, :, low], mo_s.at[1], mo_r.at[1], dev_l),
+    m_relay_l = [
+        (remote(mall.at[b_l, :, top], mall.at[b_l, :, top], mo_s.at[0], mo_r.at[0], dev_r), has_l & (chip < last)),
+        (remote(mall.at[b_l, :, low], mall.at[b_l, :, low], mo_s.at[1], mo_r.at[1], dev_r),
+         has_l & (chip < last) & (right < last)),
+    ]
+    m_relay_r = [
+        (remote(mall.at[b_r, :, top], mall.at[b_r, :, top], mo_s.at[2], mo_r.at[0], dev_l),
+         has_r & (chip < last) & (left < last)),
+        (remote(mall.at[b_r, :, low], mall.at[b_r, :, low], mo_s.at[3], mo_r.at[1], dev_l), has_r & (chip < last)),
+    ]
+    m_halves = [
+        remote(mall.at[b_o, :, top], mall.at[b_o, :, top], mo_s.at[0], mo_r.at[0], dev_r),
+        remote(mall.at[b_o, :, low], mall.at[b_o, :, low], mo_s.at[1], mo_r.at[1], dev_r),
     ]
     m_fwd = [
         remote(mall.at[b_l], mall.at[b_l], md_s.at[1], md_r.at[1], partner),
@@ -213,11 +225,24 @@
             mkv[i, :, :kv_dim] = dot(mem[...], ck[i]).astype(BF16)
             mkv[i, :, kv_dim:] = dot(mem[...], cv[i]).astype(BF16)
         mall[b_me] = mkv[...]
+    def from_left():
+        when_recv(has_l, m_own[0])
+        when_start(has_l, m_fwd[0])
+        for copy, cond in m_relay_l:
+            when_start(cond, copy)
+
+    def from_right():
+        when_recv(has_r, m_own[1])
+        when_start(has_r, m_fwd[1])
+        for copy, cond in m_relay_r:
+            when_start(cond, copy)
 
     qm[...] = jnp.zeros_like(qm)
     ones_row = (lax.broadcasted_iota(jnp.int32, (PAIR - HEAD_DIM, qc.shape[2]), 0) == 0).astype(F32).astype(BF16)
     for n in range(qc.shape[0]):
         qc[n, HEAD_DIM:] = ones_row
+    when_start(has_m, m_own[2])
+    when_start(has_m & (left < chip), m_own[1])
 
     def reset():
         m_ref[...] = jnp.full_like(m_ref, MASK_VALUE)
@@ -240,8 +265,9 @@
 
         lax.fori_loop(0, count // unroll, body, 0)
 
-    def finish(n, m):
-        val = acc[n, :, :2 * m] * (1.0 / l_ref[n, :, :2 * m])
+    def finish(n, m, first=0):
+        span = slice(first, first + 2 * m)
+        val = acc[n, :, span] * (1.0 / l_ref[n, :, span])
         return jnp.concatenate([val[:, :m], val[:, m:]], axis=0).astype(BF16).T
 
     def project_kv(pieces):
@@ -273,10 +299,13 @@
         pipelined(pairs * n_tiles, unroll, item, self_scores, self_softmax)
 
     def rest_of_layer(layer, y_rows, o_rows, m):
-        w = 2 * m
-        m_ref[:all_pairs, :, :w] = jnp.full((all_pairs, 1, w), MASK_VALUE, F32)
-        l_ref[:all_pairs, :, :w] = jnp.zeros((all_pairs, 1, w), F32)
-        acc[:all_pairs, :, :w] = jnp.zeros((all_pairs, HEAD_DIM, w), F32)
+        per = wide // (2 * m)
+        w = 2 * m * per
+        sets = all_pairs // per
+        per_group = group // per
+        m_ref[:sets, :, :w] = jnp.full((sets, 1, w), MASK_VALUE, F32)
+        l_ref[:sets, :, :w] = jnp.zeros((sets, 1, w), F32)
+        acc[:sets, :, :w] = jnp.zeros((sets, HEAD_DIM, w), F32)
         upd = dot(o_rows[0], wo[:width]) + dot(o_rows[1], wo[width:])
         y1 = (y_rows[...].astype(F32) + upd).astype(BF16)
         y_rows[...] = y1
@@ -284,31 +313,27 @@
         q_val = (dot(h, cq[...]).astype(BF16) * ATT_SCALE).astype(BF16)
         for p in range(all_pairs):
             qt = q_val[:, p * PAIR:(p + 1) * PAIR].T
-            qc[p, :HEAD_DIM, :m] = qt[:HEAD_DIM]
-            qc[p, :HEAD_DIM, m:w] = qt[HEAD_DIM:]
-
-        def chunk(c, inner):
-            off = pl.multiple_of(c * CHUNK, CHUNK)
-
-            def item(n):
-                return n // group, n
-
-            def scores(gn, buf, mc):
-                g, n = gn
-                col_scores(k_c[g, pl.ds(off, CHUNK)], qc[n, :, :w], buf, CHUNK, None, n, m_ref, mc)
-
-            def softmax(gn, buf, mc):
-                g, n = gn
-                e, alpha = col_softmax(buf, CHUNK, w, mc, n, m_ref, l_ref)
-                acc[n, :, :w] = acc[n, :, :w] * alpha + dot(vt_c[g, :, pl.ds(off, CHUNK)], e)
-
-            pipelined(all_pairs, all_pairs, item, scores, softmax)
-            return inner
-
-        lax.fori_loop(0, used * mrows // CHUNK, chunk, 0)
+            n, at = p // per, (p % per) * 2 * m
+            qc[n, :HEAD_DIM, at:at + m] = qt[:HEAD_DIM]
+            qc[n, :HEAD_DIM, at + m:at + 2 * m] = qt[HEAD_DIM:]
+
+        def item(i):
+            c, n = i // sets, lax.rem(i, sets)
+            return pl.ds(pl.multiple_of(c * CHUNK, CHUNK), CHUNK), n // per_group, n
+
+        def scores(cgn, buf, mc):
+            keys, g, n = cgn
+            col_scores(k_c[g, keys], qc[n, :, :w], buf, CHUNK, None, n, m_ref, mc)
+
+        def softmax(cgn, buf, mc):
+            keys, g, n = cgn
+            e, alpha = col_softmax(buf, CHUNK, w, mc, n, m_ref, l_ref)
+            acc[n, :, :w] = acc[n, :, :w] * alpha + dot(vt_c[g, :, keys], e)
+
+        pipelined(sets * (used * mrows // CHUNK), 6, item, scores, softmax)
         o2 = act.at[:m, :d_model]
         for p in range(all_pairs):
-            o2[:, p * PAIR:(p + 1) * PAIR] = finish(p, m)
+            o2[:, p * PAIR:(p + 1) * PAIR] = finish(p // per, m, (p % per) * 2 * m)
         y2 = (y_rows[...].astype(F32) + dot(o2[...], co[...])).astype(BF16)
         y_rows[...] = y2
         h = rms_norm(y2.astype(F32), gains[2, layer])
@@ -386,9 +411,12 @@
 
                 @pl.when(layer == 0)
                 def _():
-                    when_start(has_m, m_own[2])
                     when_start(has_m, m_own[0])
-                    when_start(has_m, m_own[1])
+                    when_start(has_m & (left > chip), m_own[1])
+
+                    @pl.when(chip < last)
+                    def _():
+                        from_right()
 
 
             @pl.when(stage == 1)
@@ -415,12 +443,11 @@
 
                 @pl.when((stage == 2) & (i == 1) & (layer == 0))
                 def _():
-                    when_recv(has_l, m_own[0])
-                    when_start(has_l, m_relay[0])
-                    when_start(has_l, m_fwd[0])
-                    when_recv(has_r, m_own[1])
-                    when_start(has_r, m_relay[1])
-                    when_start(has_r, m_fwd[1])
+                    from_left()
+
+                    @pl.when(chip == last)
+                    def _():
+                        from_right()
 
                 @pl.when(any_need & ((i == 1) | both))
                 def _():
@@ -455,17 +482,17 @@
 
         @pl.when(layer == 0)
         def _():
-            when_recv(has_o, m_relay[0])
+            when_recv(has_o, m_halves[0])
             when_start(has_o, m_fwd[2])
-            when_recv(has_o, m_relay[1])
+            when_recv(has_o, m_halves[1])
             when_start(has_o, m_fwd[3])
             when_recv(has_m, m_own[2])
             for cond, copy in zip(m_has, m_fwd):
                 when_recv(cond, copy)
             for copy in m_own:
                 when_sent(has_m, copy)
-            when_sent(has_l, m_relay[0])
-            when_sent(has_r, m_relay[1])
+            for copy, cond in (*m_relay_l, *m_relay_r):
+                when_sent(cond, copy)
             for cond, copy in zip(m_has, m_fwd):
                 when_sent(cond, copy)
 
@@ -528,7 +555,10 @@
 
         @pl.when(jnp.logical_not(gives))
         def _():
-            lax.fori_loop(0, 2, handed, 0)
+            lax.fori_loop(0, jnp.where(takes, 2, 1), handed, 0)
+
+        @pl.when(takes)
+        def _():
             back_copy.start()
             back_copy.wait_send()
 
@@ -568,7 +598,7 @@
     n_kv = cross_k.shape[2] // HEAD_DIM
     pairs, tiles = width // PAIR, 2 * rows // TILE
     combos = pairs * tiles
-    wide = max(2 * TILE, 2 * (rows - HANDED))
+    wide = 2 * (rows - HANDED)
     dma = pltpu.SemaphoreType.DMA
     return pl.pallas_call(
         functools.partial(layer_kernel, n_sp, layers),
@@ -607,7 +637,7 @@
             *[pltpu.VMEM((layers, HANDED, d_model), BF16)] * 2,
             pltpu.VMEM((2, HANDED, width), BF16),
             dma((13,)), dma((layers, 2)), *[dma((layers, 6))] * 4,
-            *[dma((2,))] * 4, *[dma((5,))] * 2, dma((layers, 2)), *[dma((layers, 3))] * 2,
+            *[dma((2,))] * 2, dma((4,)), dma((2,)), *[dma((5,))] * 2, dma((layers, 2)), *[dma((layers, 3))] * 2,
         ],
         compiler_params=pltpu.CompilerParams(collective_id=0, has_side_effects=True, vmem_limit_bytes=VMEM_LIMIT),
         name="layers",

time: 147 us -> 135 us (0.918)
  Pallas kernels: 144 us -> 132 us
    pallas_call x1, Pallas kernels: 144 us -> 132 us  [layers_call(): pl.pallas_call(functools.partial(layer_kernel, n_sp, layers), out_shape=j...]
where the time goes in v4:
time: 135 us
  Pallas kernels  132 us (98%)
  local copies, waits for them, and re-layouts  2.06 us (2%)
    pallas_call x1, Pallas kernels, layers_call(): pl.pallas_call(functools.partial(layer_kernel, n_sp, layers), out_shape=j...  132 us

profile of v4, /device:TPU:112, one launch (start us, length us, event | category | flops | bytes accessed | tf_op | source)
XLA Modules:
  0.0 135.1 jit_solution(8502573938384891572)
XLA Ops:
  0.7 132.3 %layers.1 = bf16[512,768]{1,0:T(8,128)(2,1)} custom-call(s32[1]{0:T(128)S(6)} %copy.19.len_ref, bf16[512,768]{1,0:T(8,128)(2,1)} %hid_hbm.1, bf16[256,768]{1,0:T(8,128)(2,1)} %mem_hbm.1, bf16[2,768]{1,0:T(2,128)(2,1)} %gain_s.1, bf16[2,768]{1,0:T(2,128)(2,1)} %gain_c.1, bf16[2,768]{1,0:T(2,128)(2,1)} %gain_m.1, bf16[2,768,768]{2,1,0:T(8,128)(2,1)} %wq_hbm.1, ...), custom_call_target="tpu_custom_call" | custom-call | tf_op jit(solution)/shard_map/layers/pallas_call | solution.py:603
  133.0 2.1 %copy.20 = bf16[512,768]{1,0:T(8,128)(2,1)} copy(bf16[512,768]{1,0:T(8,128)(2,1)} %layers.1) | data formatting | bytes 1572864

commit v5 on v4

--- a/solution.py
+++ b/solution.py
@@ -330,7 +330,8 @@
             e, alpha = col_softmax(buf, CHUNK, w, mc, n, m_ref, l_ref)
             acc[n, :, :w] = acc[n, :, :w] * alpha + dot(vt_c[g, :, keys], e)
 
-        pipelined(sets * (used * mrows // CHUNK), 6, item, scores, softmax)
+        count = sets * (used * mrows // CHUNK)
+        pipelined(count, count, item, scores, softmax)
         o2 = act.at[:m, :d_model]
         for p in range(all_pairs):
             o2[:, p * PAIR:(p + 1) * PAIR] = finish(p // per, m, (p % per) * 2 * m)
@@ -375,19 +376,29 @@
             key = lax.broadcasted_iota(jnp.int32, (CHUNK, 2 * TILE), 0)
             query = lax.broadcasted_iota(jnp.int32, (CHUNK, 2 * TILE), 1) % TILE
 
-            def diagonal(p, deep):
-                n = p * tiles + block * row_tiles
-                self_scores((p, n), b0, mc0, TILE, key[:TILE] <= query[:TILE])
-                self_scores((p, n + 1), b1, mc1, CHUNK, key <= query + TILE)
-                self_softmax((p, n), b0, mc0, TILE)
-                self_softmax((p, n + 1), b1, mc1, CHUNK)
-                return deep
-
-            lax.fori_loop(0, pairs, diagonal, 0)
+            order = [(p, t) for p in range(pairs) for t in range(row_tiles)]
+            bufs, mcs = (b0, b1), (mc0, mc1)
+            masks = (key[:TILE] <= query[:TILE], key <= query + TILE)
+
+            def diagonal(j, step):
+                p, t = order[j]
+                step((p, p * tiles + block * row_tiles + t), bufs[j % 2], mcs[j % 2], t)
+
+            def diagonal_scores(pn, buf, mc, t):
+                self_scores(pn, buf, mc, (t + 1) * TILE, masks[t])
+
+            def diagonal_softmax(pn, buf, mc, t):
+                self_softmax(pn, buf, mc, (t + 1) * TILE)
+
+            diagonal(0, diagonal_scores)
+            for j in range(len(order)):
+                if j + 1 < len(order):
+                    diagonal(j + 1, diagonal_scores)
+                diagonal(j, diagonal_softmax)
 
             @pl.when(block == 0)
             def _():
-                attend(tiles // 2, tiles // 2, 2)
+                attend(tiles // 2, tiles // 2, pairs * tiles // 2)
                 when_start(sent[2], ring[2])
                 when_start(sent[3], ring[3])
 
@@ -455,7 +466,7 @@
                     from_b = jnp.where(i == 1, other, core)
                     slot_b = jnp.where(both, 2 * stage + 1, 2 * stage)
                     project_kv([h_rem[layer, 2 * stage, from_a], h_rem[layer, slot_b, from_b]])
-                    attend(0, tiles, 6)
+                    attend(0, tiles, pairs * tiles)
 
                 return deep
 
@@ -489,12 +500,6 @@
             when_recv(has_m, m_own[2])
             for cond, copy in zip(m_has, m_fwd):
                 when_recv(cond, copy)
-            for copy in m_own:
-                when_sent(has_m, copy)
-            for copy, cond in (*m_relay_l, *m_relay_r):
-                when_sent(cond, copy)
-            for cond, copy in zip(m_has, m_fwd):
-                when_sent(cond, copy)
 
         mem_len = len_ref[0]
         for b in range(used):
@@ -560,31 +565,45 @@
         @pl.when(takes)
         def _():
             back_copy.start()
-            back_copy.wait_send()
 
         @pl.when(gives)
         def _():
             back_copy.wait_recv()
             y[keep:] = y_done[layer]
             next_start()
-            y_copy.wait_send()
-            o_copy.wait_send()
 
         @pl.when(layer + 1 < n_layers)
         def _():
             for copy in loads(layer + 1)[3:]:
                 copy.start()
 
+        return carry
+
+    lax.fori_loop(0, n_layers, layer_body, 0)
+    out_ref[...] = y[...]
+
+    for copy in m_own:
+        when_sent(has_m, copy)
+    for copy, cond in (*m_relay_l, *m_relay_r):
+        when_sent(cond, copy)
+    for cond, copy in zip(m_has, m_fwd):
+        when_sent(cond, copy)
+
+    def sent_all(layer, carry):
+        ring, fwd, own = row_copies(layer)
+        y_copy, o_copy, back_copy = give_copies(layer)
         own.wait_send()
-        o_send.wait_send()
+        remote(o_stage.at[layer], o_full.at[layer, core], o_sem.at[layer, 0], o_sem.at[layer, 1], partner).wait_send()
         for cond, copy in zip((*sent, relay_a, relay_b), ring):
             when_sent(cond, copy)
         for cond, copy in zip(need, fwd):
             when_sent(cond, copy)
+        when_sent(gives, y_copy)
+        when_sent(gives, o_copy)
+        when_sent(takes, back_copy)
         return carry
 
-    lax.fori_loop(0, n_layers, layer_body, 0)
-    out_ref[...] = y[...]
+    lax.fori_loop(0, n_layers, sent_all, 0)
 
 
 def layers_call(n_sp, mem_len, hidden, memory, gain_self, gain_cross, gain_mlp, self_q, self_k, self_v, self_o, cross_q,

time: 135 us -> 122 us (0.904)
  Pallas kernels: 132 us -> 119 us
    pallas_call x1, Pallas kernels: 132 us -> 119 us  [layers_call(): pl.pallas_call(functools.partial(layer_kernel, n_sp, layers), out_shape=j...]
where the time goes in v5:
time: 122 us
  Pallas kernels  119 us (98%)
  local copies, waits for them, and re-layouts  2.06 us (2%)
    pallas_call x1, Pallas kernels, layers_call(): pl.pallas_call(functools.partial(layer_kernel, n_sp, layers), out_shape=j...  119 us

profile of v5, /device:TPU:112, one launch (start us, length us, event | category | flops | bytes accessed | tf_op | source)
XLA Modules:
  0.0 122.1 jit_solution(12842430819592257643)
XLA Ops:
  0.7 119.4 %layers.1 = bf16[512,768]{1,0:T(8,128)(2,1)} custom-call(s32[1]{0:T(128)S(6)} %copy.19.len_ref, bf16[512,768]{1,0:T(8,128)(2,1)} %hid_hbm.1, bf16[256,768]{1,0:T(8,128)(2,1)} %mem_hbm.1, bf16[2,768]{1,0:T(2,128)(2,1)} %gain_s.1, bf16[2,768]{1,0:T(2,128)(2,1)} %gain_c.1, bf16[2,768]{1,0:T(2,128)(2,1)} %gain_m.1, bf16[2,768,768]{2,1,0:T(8,128)(2,1)} %wq_hbm.1, ...), custom_call_target="tpu_custom_call" | custom-call | tf_op jit(solution)/shard_map/layers/pallas_call | solution.py:622
  120.0 2.1 %copy.20 = bf16[512,768]{1,0:T(8,128)(2,1)} copy(bf16[512,768]{1,0:T(8,128)(2,1)} %layers.1) | data formatting | bytes 1572864

commit v6 on v5

--- a/solution.py
+++ b/solution.py
@@ -85,6 +85,7 @@
     last = n_chip - 1
     gives, takes = chip == last, chip == 0
     mate = 2 * (n_chip - 1 - chip) + core
+    mate_other = 2 * (n_chip - 1 - chip) + other
     keep = rows - HANDED
     wide = 2 * keep
 
@@ -110,7 +111,7 @@
         copy.start()
 
     barrier = pltpu.get_barrier_semaphore()
-    for dev in (dev_r, dev_l, partner):
+    for dev in (dev_r, dev_l, partner, mate_other):
         pl.semaphore_signal(barrier, inc=1, device_id={"sp": dev}, device_id_type=MESH)
 
     for i, ref in enumerate((gain_s, gain_c, gain_m)):
@@ -119,7 +120,7 @@
 
     first[0].wait()
     h_own[0, own_rows] = rms_norm(y[...].astype(F32), gains[0, 0])
-    pl.semaphore_wait(barrier, 3)
+    pl.semaphore_wait(barrier, 4)
 
     to_r, to_l = chip < right, chip < left
     b_to_l = to_l | (chip < opp)
@@ -147,10 +148,18 @@
         return ring, fwd, own
 
     def give_copies(layer):
+        handed_rows = pl.ds(keep, HANDED)
         return [remote(y_give.at[layer], y_take.at[layer], give_s.at[layer, 0], give_r.at[layer, 0], mate),
-                remote(o_full.at[layer, :, pl.ds(keep, HANDED)], o_take.at[layer], give_s.at[layer, 1],
-                       give_r.at[layer, 1], mate),
-                remote(y_back.at[layer], y_done.at[layer], give_s.at[layer, 2], give_r.at[layer, 2], mate)]
+                remote(y_back.at[layer], y_done.at[layer], give_s.at[layer, 1], give_r.at[layer, 1], mate),
+                remote(o_full.at[layer, core, handed_rows], o_take.at[layer, core], give_s.at[layer, 2],
+                       give_r.at[layer, 2 + core], mate),
+                remote(o_stage.at[layer, handed_rows], o_take.at[layer, core], give_s.at[layer, 3],
+                       give_r.at[layer, 2 + core], mate_other)]
+
+    def take_copies(layer):
+        rows_of = o_full.at[layer, core, pl.ds(keep, HANDED)]
+        return [remote(rows_of, o_take.at[layer, j], give_s.at[layer, 2], give_r.at[layer, 2 + j], mate)
+                for j in range(2)]
 
     def give_y(layer):
         @pl.when(gives)
@@ -343,15 +352,16 @@
             act[:m, c:c + CHUNK] = (jax.nn.silu(gate) * dot(h, wu[:, c:c + CHUNK])).astype(BF16)
         y_rows[...] = (y_rows[...].astype(F32) + dot(act[:m], wd[...])).astype(BF16)
 
+    def prepare(layer):
+        for copy in loads(layer)[:3]:
+            copy.wait()
+        wqt[...] = wq[...].T
+        wvt[...] = wv[...].T
+        reset()
+
     def layer_body(layer, carry):
         ring, fwd, own = row_copies(layer)
         weights = loads(layer)
-        reset()
-        for copy in weights[:3]:
-            copy.wait()
-        wqt[...] = wq[...].T
-        wvt[...] = wv[...].T
-
         def own_block(i, inner):
             block = jnp.where(i == 0, core, other)
 
@@ -474,15 +484,15 @@
 
         lax.fori_loop(0, 3, attend_two, 0)
 
-        for block, dst in ((other, o_stage), (core, None)):
+        for t in reversed(range(row_tiles)):
+            span = slice(t * TILE, (t + 1) * TILE)
             for p in range(pairs):
-                for t in range(row_tiles):
-                    val = finish(p * tiles + block * row_tiles + t, TILE)
-                    span = slice(t * TILE, (t + 1) * TILE)
-                    if dst is not None:
-                        dst[layer, span, p * PAIR:(p + 1) * PAIR] = val
-                    else:
-                        o_full[layer, core, span, p * PAIR:(p + 1) * PAIR] = val
+                o_stage[layer, span, p * PAIR:(p + 1) * PAIR] = finish(p * tiles + other * row_tiles + t, TILE)
+            for p in range(pairs):
+                if t == 0 and p == 1:
+                    for copy in give_copies(layer)[2:]:
+                        when_start(gives, copy)
+                o_full[layer, core, span, p * PAIR:(p + 1) * PAIR] = finish(p * tiles + core * row_tiles + t, TILE)
         o_send = remote(o_stage.at[layer], o_full.at[layer, core], o_sem.at[layer, 0], o_sem.at[layer, 1], partner)
         o_send.start()
 
@@ -514,8 +524,7 @@
                 vt_c[g, :, span] = vt[g * HEAD_DIM:(g + 1) * HEAD_DIM]
 
         o_send.wait_recv()
-        y_copy, o_copy, back_copy = give_copies(layer)
-        when_start(gives, o_copy)
+        y_copy, back_copy = give_copies(layer)[:2]
         for copy in weights[3:]:
             copy.wait()
         rest_of_layer(layer, y.at[:keep], o_full.at[layer, :, pl.ds(0, keep)], keep)
@@ -545,7 +554,8 @@
             @pl.when(i == 1)
             def _():
                 y_copy.wait_recv()
-                o_copy.wait_recv()
+                for copy in take_copies(layer):
+                    copy.wait_recv()
                 y_back[layer] = y_take[layer]
                 o_part[...] = o_take[layer]
 
@@ -565,6 +575,10 @@
         @pl.when(takes)
         def _():
             back_copy.start()
+
+        @pl.when(layer + 1 < n_layers)
+        def _():
+            prepare(layer + 1)
 
         @pl.when(gives)
         def _():
@@ -579,6 +593,7 @@
 
         return carry
 
+    prepare(0)
     lax.fori_loop(0, n_layers, layer_body, 0)
     out_ref[...] = y[...]
 
@@ -591,7 +606,7 @@
 
     def sent_all(layer, carry):
         ring, fwd, own = row_copies(layer)
-        y_copy, o_copy, back_copy = give_copies(layer)
+        y_copy, back_copy, *o_copies = give_copies(layer)
         own.wait_send()
         remote(o_stage.at[layer], o_full.at[layer, core], o_sem.at[layer, 0], o_sem.at[layer, 1], partner).wait_send()
         for cond, copy in zip((*sent, relay_a, relay_b), ring):
@@ -599,7 +614,8 @@
         for cond, copy in zip(need, fwd):
             when_sent(cond, copy)
         when_sent(gives, y_copy)
-        when_sent(gives, o_copy)
+        for copy in o_copies:
+            when_sent(gives, copy)
         when_sent(takes, back_copy)
         return carry
 
@@ -656,7 +672,7 @@
             *[pltpu.VMEM((layers, HANDED, d_model), BF16)] * 2,
             pltpu.VMEM((2, HANDED, width), BF16),
             dma((13,)), dma((layers, 2)), *[dma((layers, 6))] * 4,
-            *[dma((2,))] * 2, dma((4,)), dma((2,)), *[dma((5,))] * 2, dma((layers, 2)), *[dma((layers, 3))] * 2,
+            *[dma((2,))] * 2, dma((4,)), dma((2,)), *[dma((5,))] * 2, dma((layers, 2)), *[dma((layers, 4))] * 2,
         ],
         compiler_params=pltpu.CompilerParams(collective_id=0, has_side_effects=True, vmem_limit_bytes=VMEM_LIMIT),
         name="layers",

time: 122 us -> 121 us (level)
  no operation moved by 1% of the time
where the time goes in v6:
time: 121 us
  Pallas kernels  119 us (98%)
  local copies, waits for them, and re-layouts  2.06 us (2%)
    pallas_call x1, Pallas kernels, layers_call(): pl.pallas_call(functools.partial(layer_kernel, n_sp, layers), out_shape=j...  119 us

profile of v6, /device:TPU:112, one launch (start us, length us, event | category | flops | bytes accessed | tf_op | source)
XLA Modules:
  0.0 121.3 jit_solution(6113998199390664855)
XLA Ops:
  0.7 118.5 %layers.1 = bf16[512,768]{1,0:T(8,128)(2,1)} custom-call(s32[1]{0:T(128)S(6)} %copy.19.len_ref, bf16[512,768]{1,0:T(8,128)(2,1)} %hid_hbm.1, bf16[256,768]{1,0:T(8,128)(2,1)} %mem_hbm.1, bf16[2,768]{1,0:T(2,128)(2,1)} %gain_s.1, bf16[2,768]{1,0:T(2,128)(2,1)} %gain_c.1, bf16[2,768]{1,0:T(2,128)(2,1)} %gain_m.1, bf16[2,768,768]{2,1,0:T(8,128)(2,1)} %wq_hbm.1, ...), custom_call_target="tpu_custom_call" | custom-call | tf_op jit(solution)/shard_map/layers/pallas_call | solution.py:638
  119.2 2.1 %copy.20 = bf16[512,768]{1,0:T(8,128)(2,1)} copy(bf16[512,768]{1,0:T(8,128)(2,1)} %layers.1) | data formatting | bytes 1572864

commit v7 on v6

--- a/solution.py
+++ b/solution.py
@@ -13,6 +13,7 @@
 ATT_SCALE = HEAD_DIM ** -0.5
 MAX_MEM_LEN = 1536
 HANDED = 128
+GROUP = 1
 PAIR = 2 * HEAD_DIM
 TILE = 256
 CHUNK = 512
@@ -21,7 +22,7 @@
 F32 = jnp.float32
 BF16 = jnp.bfloat16
 MESH = pl.DeviceIdType.MESH
-VMEM_LIMIT = 60 * 1024 * 1024
+VMEM_LIMIT = 52 * 1024 * 1024
 ANY = pl.BlockSpec(memory_space=pl.ANY)
 VMEM = pl.BlockSpec(memory_space=pltpu.VMEM)
 SMEM = pl.BlockSpec(memory_space=pltpu.SMEM)
@@ -258,21 +259,16 @@
         l_ref[...] = jnp.zeros_like(l_ref)
         acc[...] = jnp.zeros_like(acc)
 
-    def pipelined(count, unroll, item, scores, softmax):
-        bufs, mcs = (b0, b1), (mc0, mc1)
-
-        def at(i):
-            return item(jnp.minimum(i, count - 1))
-
-        scores(at(0), b0, mc0)
-
-        def body(i, carry):
-            for u in range(unroll):
-                scores(at(unroll * i + u + 1), bufs[(u + 1) % 2], mcs[(u + 1) % 2])
-                softmax(at(unroll * i + u), bufs[u % 2], mcs[u % 2])
-            return carry
-
-        lax.fori_loop(0, count // unroll, body, 0)
+    def pipelined(count, item, scores, softmax, together=1):
+        def place(i):
+            k, v = (i // together) % 2, i % together
+            return (b0, b1)[k].at[v], (mc0, mc1)[k].at[v]
+
+        for i in range(-together, count, together):
+            for j in range(i + together, min(i + 2 * together, count)):
+                scores(item(j), *place(j))
+            for j in range(max(i, 0), i + together):
+                softmax(item(j), *place(j))
 
     def finish(n, m, first=0):
         span = slice(first, first + 2 * m)
@@ -300,12 +296,12 @@
         acc[n, :, :TILE] = acc[n, :, :TILE] * alpha[:, :TILE] + dot(vt_s[p, :HEAD_DIM, :size], e[:, :TILE])
         acc[n, :, TILE:w] = acc[n, :, TILE:w] * alpha[:, TILE:] + dot(vt_s[p, HEAD_DIM:, :size], e[:, TILE:])
 
-    def attend(first_tile, n_tiles, unroll):
+    def attend(first_tile, n_tiles):
         def item(i):
             p = i // n_tiles
-            return p, p * tiles + first_tile + lax.rem(i, n_tiles)
-
-        pipelined(pairs * n_tiles, unroll, item, self_scores, self_softmax)
+            return p, p * tiles + first_tile + i % n_tiles
+
+        pipelined(pairs * n_tiles, item, self_scores, self_softmax, GROUP)
 
     def rest_of_layer(layer, y_rows, o_rows, m):
         per = wide // (2 * m)
@@ -327,8 +323,8 @@
             qc[n, :HEAD_DIM, at + m:at + 2 * m] = qt[HEAD_DIM:]
 
         def item(i):
-            c, n = i // sets, lax.rem(i, sets)
-            return pl.ds(pl.multiple_of(c * CHUNK, CHUNK), CHUNK), n // per_group, n
+            c, n = i // sets, i % sets
+            return pl.ds(c * CHUNK, CHUNK), n // per_group, n
 
         def scores(cgn, buf, mc):
             keys, g, n = cgn
@@ -340,7 +336,7 @@
             acc[n, :, :w] = acc[n, :, :w] * alpha + dot(vt_c[g, :, keys], e)
 
         count = sets * (used * mrows // CHUNK)
-        pipelined(count, count, item, scores, softmax)
+        pipelined(count, item, scores, softmax)
         o2 = act.at[:m, :d_model]
         for p in range(all_pairs):
             o2[:, p * PAIR:(p + 1) * PAIR] = finish(p // per, m, (p % per) * 2 * m)
@@ -387,12 +383,11 @@
             query = lax.broadcasted_iota(jnp.int32, (CHUNK, 2 * TILE), 1) % TILE
 
             order = [(p, t) for p in range(pairs) for t in range(row_tiles)]
-            bufs, mcs = (b0, b1), (mc0, mc1)
             masks = (key[:TILE] <= query[:TILE], key <= query + TILE)
 
             def diagonal(j, step):
                 p, t = order[j]
-                step((p, p * tiles + block * row_tiles + t), bufs[j % 2], mcs[j % 2], t)
+                step((p, p * tiles + block * row_tiles + t), (b0, b1)[j % 2].at[0], (mc0, mc1)[j % 2].at[0], t)
 
             def diagonal_scores(pn, buf, mc, t):
                 self_scores(pn, buf, mc, (t + 1) * TILE, masks[t])
@@ -408,7 +403,7 @@
 
             @pl.when(block == 0)
             def _():
-                attend(tiles // 2, tiles // 2, pairs * tiles // 2)
+                attend(tiles // 2, tiles // 2)
                 when_start(sent[2], ring[2])
                 when_start(sent[3], ring[3])
 
@@ -476,7 +471,7 @@
                     from_b = jnp.where(i == 1, other, core)
                     slot_b = jnp.where(both, 2 * stage + 1, 2 * stage)
                     project_kv([h_rem[layer, 2 * stage, from_a], h_rem[layer, slot_b, from_b]])
-                    attend(0, tiles, pairs * tiles)
+                    attend(0, tiles)
 
                 return deep
 
@@ -661,8 +656,8 @@
             pltpu.VMEM((n_kv, HEAD_DIM, used * mrows), BF16),
             *[pltpu.VMEM((combos, 1, wide), F32)] * 2,
             pltpu.VMEM((combos, HEAD_DIM, wide), F32),
-            *[pltpu.VMEM((CHUNK, wide), F32)] * 2,
-            *[pltpu.VMEM((1, wide), F32)] * 2,
+            *[pltpu.VMEM((GROUP, CHUNK, wide), F32)] * 2,
+            *[pltpu.VMEM((GROUP, 1, wide), F32)] * 2,
             pltpu.VMEM((layers, rows, width), BF16),
             pltpu.VMEM((layers, 2, rows, width), BF16),
             pltpu.VMEM((rows, ff), BF16),

time: 121 us -> 124 us (1.025)
  local copies, waits for them, and re-layouts: 2.06 us -> 5.91 us
    unnamed x1 -> x13, local copies, waits for them, and re-layouts: 2.06 us -> 5.91 us
where the time goes in v7:
time: 124 us
  Pallas kernels  118 us (95%)
  local copies, waits for them, and re-layouts  5.91 us (5%)
    pallas_call x1, Pallas kernels, layers_call(): pl.pallas_call(functools.partial(layer_kernel, n_sp, layers), out_shape=j...  118 us
    unnamed x13, local copies, waits for them, and re-layouts  5.91 us

profile of v7, /device:TPU:112, one launch (start us, length us, event | category | flops | bytes accessed | tf_op | source)
XLA Modules:
  0.0 124.2 jit_solution(10408497348822164166)
XLA Ops:
  0.7 0.0 copy-start
  0.7 1.0 copy-done
  1.6 0.0 copy-start.1
  1.7 1.0 copy-done.1
  2.6 0.0 copy-start.2
  2.6 1.0 copy-done.2
  3.6 0.0 copy-start.3
  3.6 0.7 copy-done.3
  4.3 0.0 copy-start.4
  4.3 0.7 copy-done.4
  5.0 0.0 copy-start.5
  5.0 0.7 copy-done.5
  5.7 117.6 %layers.1 = bf16[512,768]{1,0:T(8,128)(2,1)S(1)} custom-call(s32[1]{0:T(128)S(6)} %copy.19.len_ref, bf16[512,768]{1,0:T(8,128)(2,1)} %hid_hbm.1, bf16[256,768]{1,0:T(8,128)(2,1)S(1)} %copy-done, bf16[2,768]{1,0:T(2,128)(2,1)S(1)} %copy-done.3, bf16[2,768]{1,0:T(2,128)(2,1)S(1)} %copy-done.4, bf16[2,768]{1,0:T(2,128)(2,1)S(1)} %copy-done.5, ...), custom_call_target="tpu_custom_call" | custom-call | tf_op jit(solution)/shard_map/layers/pallas_call | solution.py:633
  123.3 0.9 copy.20
Async XLA Ops:
  0.7 1.0 copy-start
  1.6 1.0 copy-start.1
  2.6 1.0 copy-start.2
  3.6 0.7 copy-start.3
  4.3 0.7 copy-start.4
  5.0 0.7 copy-start.5

commit v8 on v7

--- a/solution.py
+++ b/solution.py
@@ -23,7 +23,7 @@
 BF16 = jnp.bfloat16
 MESH = pl.DeviceIdType.MESH
 VMEM_LIMIT = 52 * 1024 * 1024
-ANY = pl.BlockSpec(memory_space=pl.ANY)
+HBM = pl.BlockSpec(memory_space=pltpu.HBM)
 VMEM = pl.BlockSpec(memory_space=pltpu.VMEM)
 SMEM = pl.BlockSpec(memory_space=pltpu.SMEM)
 
@@ -58,7 +58,7 @@
 def layer_kernel(n_sp, n_layers, len_ref, hid_hbm, mem_hbm, gain_s, gain_c, gain_m, wq_hbm, wk_hbm, wv_hbm, wo_hbm, cq_hbm,
                  ck_hbm, cv_hbm, co_hbm, wg_hbm, wu_hbm, wd_hbm, out_ref,
                  y, h_own, h_rem, mem, ck, cv, mkv, mall, wq, wk, wv, wqt, wvt, wo, cq, co, wg, wu, wd,
-                 qm, qc, k_s, vt_s, k_c, vt_c, m_ref, l_ref, acc, b0, b1, mc0, mc1, o_stage, o_full, act, gains,
+                 qm, qc, k_s, vt_s, k_c, vt_c, m_ref, l_ref, acc, b0, b1, mc0, mc1, o_stage, o_full, act, gains, gain_in,
                  y_give, y_take, o_take, y_back, y_done, o_part,
                  w_sem, own_sem, ici_s, ici_r, d2d_s, d2d_r, mi_s, mi_r, mo_s, mo_r, md_s, md_r, o_sem,
                  give_s, give_r):
@@ -107,6 +107,9 @@
     first = [pltpu.make_async_copy(src, dst, w_sem.at[9 + i])
              for i, (src, dst) in enumerate(((hid_hbm, y), (mem_hbm, mem), (ck_hbm, ck), (cv_hbm, cv)))]
     first[0].start()
+    gain_loads = [pltpu.make_async_copy(src, gain_in.at[i], w_sem.at[13 + i]) for i, src in enumerate((gain_s, gain_c, gain_m))]
+    for copy in gain_loads:
+        copy.start()
     w_first = loads(0)
     for copy in (*w_first[:3], *first[1:], *w_first[3:]):
         copy.start()
@@ -115,9 +118,11 @@
     for dev in (dev_r, dev_l, partner, mate_other):
         pl.semaphore_signal(barrier, inc=1, device_id={"sp": dev}, device_id_type=MESH)
 
-    for i, ref in enumerate((gain_s, gain_c, gain_m)):
+    for copy in gain_loads:
+        copy.wait()
+    for i in range(3):
         for j in range(n_layers):
-            gains[i, j] = ref[j:j + 1].astype(F32)
+            gains[i, j] = gain_in[i, j:j + 1].astype(F32)
 
     first[0].wait()
     h_own[0, own_rows] = rms_norm(y[...].astype(F32), gains[0, 0])
@@ -633,7 +638,7 @@
     return pl.pallas_call(
         functools.partial(layer_kernel, n_sp, layers),
         out_shape=jax.ShapeDtypeStruct((rows, d_model), BF16),
-        in_specs=[SMEM, ANY, ANY, VMEM, VMEM, VMEM] + [ANY] * 11,
+        in_specs=[SMEM] + [HBM] * 16,
         out_specs=VMEM,
         scratch_shapes=[
             pltpu.VMEM((rows, d_model), BF16),
@@ -662,17 +667,19 @@
             pltpu.VMEM((layers, 2, rows, width), BF16),
             pltpu.VMEM((rows, ff), BF16),
             pltpu.VMEM((3, layers, 1, d_model), F32),
+            pltpu.VMEM((3, layers, d_model), BF16),
             *[pltpu.VMEM((layers, HANDED, d_model), BF16)] * 2,
             pltpu.VMEM((layers, 2, HANDED, width), BF16),
             *[pltpu.VMEM((layers, HANDED, d_model), BF16)] * 2,
             pltpu.VMEM((2, HANDED, width), BF16),
-            dma((13,)), dma((layers, 2)), *[dma((layers, 6))] * 4,
+            dma((16,)), dma((layers, 2)), *[dma((layers, 6))] * 4,
             *[dma((2,))] * 2, dma((4,)), dma((2,)), *[dma((5,))] * 2, dma((layers, 2)), *[dma((layers, 4))] * 2,
         ],
         compiler_params=pltpu.CompilerParams(collective_id=0, has_side_effects=True, vmem_limit_bytes=VMEM_LIMIT),
         name="layers",
-    )(mem_len, hidden, memory, gain_self, gain_cross, gain_mlp, self_q, self_k, self_v, self_o, cross_q, cross_k, cross_v,
-      cross_o, gate, up, down)
+    )(mem_len, *[pltpu.with_memory_space_constraint(x, pltpu.HBM) for x in (
+        hidden, memory, gain_self, gain_cross, gain_mlp, self_q, self_k, self_v, self_o, cross_q, cross_k, cross_v, cross_o,
+        gate, up, down)])
 
 
 def solution(mesh):

time: 124 us -> 119 us (0.960)
  local copies, waits for them, and re-layouts: 5.91 us -> 0.88 us
    unnamed x13 -> x1, local copies, waits for them, and re-layouts: 5.91 us -> 0.88 us
where the time goes in v8:
time: 119 us
  Pallas kernels  117 us (98%)
    pallas_call x1, Pallas kernels, layers_call(): pl.pallas_call(functools.partial(layer_kernel, n_sp, layers), out_shape=j...  117 us

profile of v8, /device:TPU:112, one launch (start us, length us, event | category | flops | bytes accessed | tf_op | source)
XLA Modules:
  0.0 118.7 jit_solution(12608977071096128026)
XLA Ops:
  0.7 117.1 %layers.1 = bf16[512,768]{1,0:T(8,128)(2,1)S(1)} custom-call(s32[1]{0:T(128)S(6)} %copy.19.len_ref, bf16[512,768]{1,0:T(8,128)(2,1)} %hid_hbm.1, bf16[256,768]{1,0:T(8,128)(2,1)} %mem_hbm.1, bf16[2,768]{1,0:T(2,128)(2,1)} %gain_s.1, bf16[2,768]{1,0:T(2,128)(2,1)} %gain_c.1, bf16[2,768]{1,0:T(2,128)(2,1)} %gain_m.1, bf16[2,768,768]{2,1,0:T(8,128)(2,1)} %wq_hbm.1, ...), custom_call_target="tpu_custom_call" | custom-call | tf_op jit(solution)/shard_map/layers/pallas_call | solution.py:638
  117.8 0.9 copy.20
